TPU v7x, 128 devices: a whole 4x4x4 slice. The times are simulated.
128 devices in a mesh: gx: 8 (over y, core), gy: 16 (over x, z).
Axes of the slice: x: 4, y: 4, z: 4, core: 2. Of those that a mesh axis runs over, the one named last changes fastest.
Arguments:
- right_side: float32 [256, 512, 512], P('gx', 'gy'), as said below
- start_guess: float32 [256, 512, 512], P('gx', 'gy'), may hold values from -3 to 3
- conductivity: float32 [256, 512, 512], P('gx', 'gy'), may hold values from 0.5 to 8
Outputs:
- solution_field: float32 [256, 512, 512], P('gx', 'gy')
- estimate: float32 [], replicated
Inputs may be any that keep to these rules, and one draw needn't show every extreme that they name: `right_side`: A smoothly varying positive scale times noise, which may have a nonzero mean.
All inputs are finite; a program needn't handle non-finite values.
Results may differ from a plain program's by a relative error of at most 0.0003.
Values sent between devices are 32-bit elements; how exact they have to be, the bound alone decides.
A program may use at most 64 MiB of HBM per device.

v0:
```python
import jax
import jax.numpy as jnp
from jax import lax
from jax.sharding import Mesh
from jax.sharding import PartitionSpec as P

M = 3
GX_GY = ("gx_0", "gx_1", "gy_0", "gy_1")
GX = ("gx_0", "gx_1")
GY = ("gy_0", "gy_1")


def with_halo(x, sides, width):
    edges = {}
    for axis, dim in sides:
        devices, length = (lax.axis_size(axis), x.shape[dim])
        up = [(i, (i + 1) % devices) for i in range(devices - 1)]
        last = lax.slice_in_dim(x, length - width, length, axis=dim)
        initial = lax.slice_in_dim(x, 0, width, axis=dim)
        edges[dim] = (
            lax.ppermute(last, axis, up),
            lax.ppermute(initial, axis, [(b, a) for a, b in up]),
        )
    done = []
    for _, dim in sides:
        low, high = edges[dim]
        around = [(width, width) if d in done else (0, 0) for d in range(x.ndim)]
        x = jnp.concatenate([jnp.pad(low, around), x, jnp.pad(high, around)], axis=dim)
        done.append(dim)
    return x


def over_axes(x, axes):
    for axis in axes:
        x = lax.psum(x, axis)
    return x


def shifted(padded, which, sign):
    starts = [1, 1, 1]
    starts[which] = 1 + sign
    limits = [starts[dim] + padded.shape[dim] - 2 for dim in range(3)]
    return lax.slice(padded, starts, limits)


def extend_z(padded):
    return jnp.pad(padded, ((0, 0), (0, 0), (1, 1)))


def stencil(field, kappa_pad):
    padded = extend_z(with_halo(field, ((GX, 0), (GY, 1)), 1))
    centre = shifted(padded, 0, 0)
    middle = shifted(kappa_pad, 0, 0)
    result = jnp.zeros_like(centre)
    for which in range(3):
        for sign in (-1, 1):
            result = result + 0.5 * (middle + shifted(kappa_pad, which, sign)) * (
                centre - shifted(padded, which, sign)
            )
    return result


def global_norm(vector):
    return jnp.sqrt(over_axes(jnp.sum(vector * vector), GX_GY))


def least_squares(columns, beta):
    count = len(columns)
    rhs_vals = [beta] + [jnp.float32(0.0)] * count
    cosines = []
    sines = []
    upper = []
    for column in range(count):
        entries = list(columns[column])
        for earlier in range(column):
            first = entries[earlier]
            second = entries[earlier + 1]
            entries[earlier] = cosines[earlier] * first + sines[earlier] * second
            entries[earlier + 1] = -sines[earlier] * first + cosines[earlier] * second
        first = entries[column]
        second = entries[column + 1]
        radius = jnp.sqrt(first * first + second * second)
        cosines.append(first / radius)
        sines.append(second / radius)
        entries[column] = radius
        rhs_vals[column + 1] = -sines[column] * rhs_vals[column]
        rhs_vals[column] = cosines[column] * rhs_vals[column]
        upper.append(entries[: column + 1])
    coeffs = [None] * count
    for row in reversed(range(count)):
        value = rhs_vals[row]
        for later in range(row + 1, count):
            value = value - upper[later][row] * coeffs[later]
        coeffs[row] = value / upper[row][row]
    return (coeffs, jnp.abs(rhs_vals[count]))


def local(right_side, start_guess, conductivity):
    kappa_pad = extend_z(with_halo(conductivity, ((GX, 0), (GY, 1)), 1))
    start = right_side - stencil(start_guess, kappa_pad)
    beta = global_norm(start)
    basis = [start / beta]
    columns = []
    for column in range(M):
        vector = stencil(basis[column], kappa_pad)
        local_dots = jnp.stack([jnp.sum(vector * basis[earlier]) for earlier in range(column + 1)])
        coeff_all, squares = (
            over_axes(local_dots, GX_GY),
            over_axes(jnp.sum(vector * vector), GX_GY),
        )
        for earlier in range(column + 1):
            vector = vector - coeff_all[earlier] * basis[earlier]
        entries = [coeff_all[earlier] for earlier in range(column + 1)]
        length = jnp.sqrt(squares - jnp.sum(coeff_all * coeff_all))
        entries.append(length)
        columns.append(entries)
        basis.append(vector / length)
    coeffs, estimate = least_squares(columns, beta)
    solution_field = start_guess
    for column in range(M):
        solution_field = solution_field + coeffs[column] * basis[column]
    return (solution_field, estimate)


def solution(mesh):
    split = Mesh(mesh.devices.reshape(4, 2, 4, 4), ("gx_0", "gx_1", "gy_0", "gy_1"))
    return jax.shard_map(
        local,
        mesh=split,
        in_specs=(P(GX, GY, None), P(GX, GY, None), P(GX, GY, None)),
        out_specs=(P(GX, GY, None), P()),
        check_vma=False,
    )
```

profile of v0, /device:TPU:1, one launch (start us, length us, event | category | flops | bytes accessed | tf_op | source)
XLA Modules:
  0.0 295.1 jit_solution(9819572107874024284)
XLA Ops:
  0.6 0.9 fusion.82
  1.5 4.6 %collective-permute-start = (f32[1,32,512]{2,1,0:T(8,128)S(1)}, f32[1,32,512]{2,1,0:T(8,128)S(1)}, u32[]{:S(2)}, u32[]{:S(2)}) collective-permute-start(f32[1,32,512]{2,1,0:T(8,128)S(1)} %get-tuple-element.54), channel_id=1, source_target_pairs={{0,16},{16,32},{32,48},{48,64},{64,80},{80,96},{96,112},{1,17},{17... | collective-permute-start | bytes 196616 | tf_op jit(solution)/shard_map/ppermute | solution.py:21
  6.1 1.9 collective-permute-start.2
  8.0 1.3 fusion.81
  9.4 3.5 %collective-permute-start.4 = (f32[32,1,512]{2,1,0:T(1,128)S(1)}, f32[32,1,512]{2,1,0:T(1,128)S(1)}, u32[]{:S(2)}, u32[]{:S(2)}) collective-permute-start(f32[32,1,512]{2,1,0:T(1,128)S(1)} %get-tuple-element.51), channel_id=1, source_target_pairs={{0,1},{1,2},{2,3},{3,4},{4,5},{5,6},{6,7},{7,8},{8,9},{9,10},{10,1... | collective-permute-start | bytes 196616 | tf_op jit(solution)/shard_map/ppermute | solution.py:21
  12.9 1.3 collective-permute-start.6
  14.2 0.9 fusion.84
  15.1 3.9 %collective-permute-start.1 = (f32[1,32,512]{2,1,0:T(8,128)S(1)}, f32[1,32,512]{2,1,0:T(8,128)S(1)}, u32[]{:S(2)}, u32[]{:S(2)}) collective-permute-start(f32[1,32,512]{2,1,0:T(8,128)S(1)} %get-tuple-element.58), channel_id=1, source_target_pairs={{0,16},{16,32},{32,48},{48,64},{64,80},{80,96},{96,112},{1,17},{17... | collective-permute-start | bytes 196616 | tf_op jit(solution)/shard_map/ppermute | solution.py:21
  19.0 1.3 fusion.83
  20.4 1.9 collective-permute-start.3
  22.3 1.8 constant_dynamic-update-slice_fusion.1
  24.1 4.3 %collective-permute-start.5 = (f32[32,1,512]{2,1,0:T(1,128)S(1)}, f32[32,1,512]{2,1,0:T(1,128)S(1)}, u32[]{:S(2)}, u32[]{:S(2)}) collective-permute-start(f32[32,1,512]{2,1,0:T(1,128)S(1)} %get-tuple-element.55), channel_id=1, source_target_pairs={{0,1},{1,2},{2,3},{3,4},{4,5},{5,6},{6,7},{7,8},{8,9},{9,10},{10,1... | collective-permute-start | bytes 196616 | tf_op jit(solution)/shard_map/ppermute | solution.py:21
  28.5 1.3 collective-permute-start.7
  29.9 1.6 select_maximum_fusion.14
  31.5 0.8 copy-done.11
  32.5 1.1 collective-permute-done.7
  33.7 1.6 select_maximum_fusion.12
  35.4 8.7 %multiply_reduce_fusion.9 = (f32[]{:T(128)}, f32[32,32,512]{2,1,0:T(8,128)}) fusion(f32[32,32,512]{2,1,0:T(8,128)} %param.3, f32[32,32,512]{2,1,0:T(8,128)S(1)} %copy-done.11, f32[34,34,514]{2,1,0:T(8,128)S(1)} %select_maximum_fusion.12, f32[32,32,512]{2,1,0:T(8,128)S(1)} %copy-done.7, f32[34,34,514]{2,1,0:T(8,128)S(1)} %select_maximum_fusion.14, ...), kind=kLoop, calls=%fused_computation.144 | loop fusion | flops 20971520 | bytes 21774340 | tf_op jit(solution)/shard_map/reduce_sum | solution.py:64
  44.1 8.1 %psum.196 = f32[]{:T(128)} all-reduce(f32[]{:T(128)} %get-tuple-element.37), channel_id=1, replica_groups=mesh['gx_0'=4,'gx_1'=2,'gy_0'=4,'gy_1'=4] {'gx_0'}, use_global_device_ids=true, to_apply=%region_1.2 | all-reduce | flops 1 | bytes 8 | tf_op jit(solution)/shard_map/psum | solution.py:35
  52.2 7.7 %psum.197 = f32[]{:T(128)} all-reduce(f32[]{:T(128)} %psum.196), channel_id=1, replica_groups=mesh['gx_0'=4,'gx_1'=2,'gy_0'=4,'gy_1'=4] {'gx_1'}, use_global_device_ids=true, to_apply=%region_2.3 | all-reduce | flops 1 | bytes 8 | tf_op jit(solution)/shard_map/psum | solution.py:35
  60.0 12.1 %psum.198 = f32[]{:T(128)} all-reduce(f32[]{:T(128)} %psum.197), channel_id=1, replica_groups=mesh['gx_0'=4,'gx_1'=2,'gy_0'=4,'gy_1'=4] {'gy_0'}, use_global_device_ids=true, to_apply=%region_3.4 | all-reduce | flops 1 | bytes 8 | tf_op jit(solution)/shard_map/psum | solution.py:35
  72.1 8.7 %psum.199 = f32[]{:T(128)} all-reduce(f32[]{:T(128)} %psum.198), channel_id=1, replica_groups=mesh['gx_0'=4,'gx_1'=2,'gy_0'=4,'gy_1'=4] {'gy_1'}, use_global_device_ids=true, to_apply=%region_4.5 | all-reduce | flops 1 | bytes 8 | tf_op jit(solution)/shard_map/psum | solution.py:35
  81.5 1.8 broadcast_divide_fusion
  83.5 1.3 collective-permute-start.10
  84.8 1.3 collective-permute-start.11
  86.1 5.7 %collective-permute-start.8 = (f32[1,32,512]{2,1,0:T(8,128)S(1)}, f32[1,32,512]{2,1,0:T(8,128)S(1)}, u32[]{:S(2)}, u32[]{:S(2)}) collective-permute-start(f32[1,32,512]{2,1,0:T(8,128)S(1)} %get-tuple-element.47), channel_id=1, source_target_pairs={{0,16},{16,32},{32,48},{48,64},{64,80},{80,96},{96,112},{1,17},{17... | collective-permute-start | bytes 196616 | tf_op jit(solution)/shard_map/ppermute | solution.py:21
  91.7 2.2 collective-permute-start.9
  94.1 3.2 %collective-permute-done.9 = f32[1,32,512]{2,1,0:T(8,128)S(1)} collective-permute-done((f32[1,32,512]{2,1,0:T(8,128)S(1)}, f32[1,32,512]{2,1,0:T(8,128)S(1)}, u32[]{:S(2)}, u32[]{:S(2)}) %collective-permute-start.9) | collective-permute-done | bytes 65568 | tf_op jit(solution)/shard_map/ppermute | solution.py:22
  97.3 3.3 %select_maximum_fusion.8 = f32[34,34,514]{2,1,0:T(8,128)S(1)} fusion(f32[34,1,512]{2,1,0:T(1,128)S(1)} %pad.54, f32[34,1,512]{2,1,0:T(1,128)S(1)} %pad.53, f32[1,32,512]{2,1,0:T(8,128)S(1)} %collective-permute-done.9, f32[32,32,512]{2,1,0:T(8,128)S(1)} %broadcast_divide_fusion, f32[1,32,512]{2,1,0:T(8,128)S(1)} %collective-permute-done.8), kind=kLoop, calls=%fused_computation.10 | loop fusion | flops 7130208 | bytes 4744224 | tf_op jit(solution)/shard_map/concatenate | solution.py:28
  100.7 9.1 %multiply_reduce_fusion.8 = (f32[]{:T(128)}, f32[]{:T(128)}, f32[32,32,512]{2,1,0:T(8,128)}) fusion(f32[32,32,512]{2,1,0:T(8,128)S(1)} %broadcast_divide_fusion, f32[34,34,514]{2,1,0:T(8,128)S(1)} %select_maximum_fusion.8, f32[32,32,512]{2,1,0:T(8,128)S(1)} %copy-done.8, f32[34,34,514]{2,1,0:T(8,128)S(1)} %select_maximum_fusion.14, ...), kind=kLoop, calls=%fused_computation.143 | loop fusion | flops 23592960 | bytes 17448968 | tf_op jit(solution)/shard_map/reduce_sum | solution.py:106
  109.7 7.7 %all-reduce.23 = (f32[]{:T(128)}, f32[1]{0:T(128)}) all-reduce(f32[]{:T(128)} %get-tuple-element.10, f32[1]{0:T(128)} %bitcast), channel_id=1, replica_groups=mesh['gx_0'=4,'gx_1'=2,'gy_0'=4,'gy_1'=4] {'gx_0'}, use_global_device_ids=true, to_apply=%region_11.12 | all-reduce | flops 2 | bytes 16 | tf_op jit(solution)/shard_map/psum | solution.py:35
  117.4 4.0 %all-reduce.26 = (f32[]{:T(128)}, f32[1]{0:T(128)}) all-reduce(f32[]{:T(128)} %get-tuple-element.27, f32[1]{0:T(128)} %get-tuple-element.28), channel_id=1, replica_groups=mesh['gx_0'=4,'gx_1'=2,'gy_0'=4,'gy_1'=4] {'gx_1'}, use_global_device_ids=true, to_apply=%region_12.13 | all-reduce | flops 2 | bytes 16 | tf_op jit(solution)/shard_map/psum | solution.py:35
  121.4 12.0 %all-reduce.20 = (f32[]{:T(128)}, f32[1]{0:T(128)}) all-reduce(f32[]{:T(128)} %get-tuple-element.33, f32[1]{0:T(128)} %get-tuple-element.34), channel_id=1, replica_groups=mesh['gx_0'=4,'gx_1'=2,'gy_0'=4,'gy_1'=4] {'gy_0'}, use_global_device_ids=true, to_apply=%region_13.14 | all-reduce | flops 2 | bytes 16 | tf_op jit(solution)/shard_map/psum | solution.py:35
  133.4 6.6 %all-reduce.17 = (f32[]{:T(128)}, f32[1]{0:T(128)}) all-reduce(f32[]{:T(128)} %get-tuple-element.21, f32[1]{0:T(128)} %get-tuple-element.22), channel_id=1, replica_groups=mesh['gx_0'=4,'gx_1'=2,'gy_0'=4,'gy_1'=4] {'gy_1'}, use_global_device_ids=true, to_apply=%region_14.15 | all-reduce | flops 2 | bytes 16 | tf_op jit(solution)/shard_map/psum | solution.py:35
  142.0 3.4 %subtract_divide_fusion.1 = f32[32,32,512]{2,1,0:T(8,128)S(1)} fusion(f32[32,32,512]{2,1,0:T(8,128)} %get-tuple-element.36, f32[]{:T(128)S(6)} %sqrt.22, f32[]{:T(128)} %bitcast.1, f32[32,32,512]{2,1,0:T(8,128)} %get-tuple-element.38, f32[]{:T(128)S(6)} %sqrt.21), kind=kLoop, calls=%fused_computation.141 | loop fusion | flops 2097152 | bytes 6291468 | tf_op jit(solution)/shard_map/div | solution.py:117
  145.5 3.6 %collective-permute-start.14 = (f32[32,1,512]{2,1,0:T(1,128)S(1)}, f32[32,1,512]{2,1,0:T(1,128)S(1)}, u32[]{:S(2)}, u32[]{:S(2)}) collective-permute-start(f32[32,1,512]{2,1,0:T(1,128)S(1)} %get-tuple-element.45), channel_id=1, source_target_pairs={{0,1},{1,2},{2,3},{3,4},{4,5},{5,6},{6,7},{7,8},{8,9},{9,10},{10,1... | collective-permute-start | bytes 196616 | tf_op jit(solution)/shard_map/ppermute | solution.py:21
  149.2 1.3 collective-permute-start.15
  150.5 6.6 %collective-permute-start.12 = (f32[1,32,512]{2,1,0:T(8,128)S(1)}, f32[1,32,512]{2,1,0:T(8,128)S(1)}, u32[]{:S(2)}, u32[]{:S(2)}) collective-permute-start(f32[1,32,512]{2,1,0:T(8,128)S(1)} %get-tuple-element.43), channel_id=1, source_target_pairs={{0,16},{16,32},{32,48},{48,64},{64,80},{80,96},{96,112},{1,17},{17... | collective-permute-start | bytes 196616 | tf_op jit(solution)/shard_map/ppermute | solution.py:21
  157.1 1.9 collective-permute-start.13
  159.2 3.5 %collective-permute-done.13 = f32[1,32,512]{2,1,0:T(8,128)S(1)} collective-permute-done((f32[1,32,512]{2,1,0:T(8,128)S(1)}, f32[1,32,512]{2,1,0:T(8,128)S(1)}, u32[]{:S(2)}, u32[]{:S(2)}) %collective-permute-start.13) | collective-permute-done | bytes 65568 | tf_op jit(solution)/shard_map/ppermute | solution.py:22
  162.7 3.3 %select_maximum_fusion.4 = f32[34,34,514]{2,1,0:T(8,128)S(1)} fusion(f32[34,1,512]{2,1,0:T(1,128)S(1)} %pad.57, f32[34,1,512]{2,1,0:T(1,128)S(1)} %pad.56, f32[1,32,512]{2,1,0:T(8,128)S(1)} %collective-permute-done.13, f32[32,32,512]{2,1,0:T(8,128)S(1)} %subtract_divide_fusion.1, f32[1,32,512]{2,1,0:T(8,128)S(1)} %collective-permute-done.12), kind=kLoop, calls=%fused_computation.6 | loop fusion | flops 7130208 | bytes 4744224 | tf_op jit(solution)/shard_map/concatenate | solution.py:28
  166.1 9.2 %multiply_reduce_fusion.6 = (f32[]{:T(128)}, f32[]{:T(128)}, f32[]{:T(128)}, f32[32,32,512]{2,1,0:T(8,128)}) fusion(f32[32,32,512]{2,1,0:T(8,128)S(1)} %subtract_divide_fusion.1, f32[34,34,514]{2,1,0:T(8,128)S(1)} %select_maximum_fusion.4, f32[32,32,512]{2,1,0:T(8,128)S(1)} %copy-done.9, f32[34,34,514]{2,1,0:T(8,128)S(1)} %select_maximum_fusion.14, ...), kind=kLoop, calls=%fused_computation.140 | loop fusion | flops 25165824 | bytes 19546128 | tf_op jit(solution)/shard_map/reduce_sum | solution.py:106
  175.3 1.3 pad_maximum_fusion.32
  176.6 6.7 %all-reduce.22 = (f32[]{:T(128)}, f32[2]{0:T(128)}) all-reduce(f32[]{:T(128)} %get-tuple-element.7, f32[2]{0:T(128)S(1)} %pad_maximum_fusion.32), channel_id=1, replica_groups=mesh['gx_0'=4,'gx_1'=2,'gy_0'=4,'gy_1'=4] {'gx_0'}, use_global_device_ids=true, to_apply=%region_22.23 | all-reduce | flops 3 | bytes 24 | tf_op jit(solution)/shard_map/psum | solution.py:35
  183.4 4.8 %all-reduce.25 = (f32[]{:T(128)}, f32[2]{0:T(128)S(1)}) all-reduce(f32[]{:T(128)} %get-tuple-element.25, f32[2]{0:T(128)} %get-tuple-element.26), channel_id=1, replica_groups=mesh['gx_0'=4,'gx_1'=2,'gy_0'=4,'gy_1'=4] {'gx_1'}, use_global_device_ids=true, to_apply=%region_23.24 | all-reduce | flops 3 | bytes 24 | tf_op jit(solution)/shard_map/psum | solution.py:35
  188.2 10.5 %all-reduce.19 = (f32[]{:T(128)}, f32[2]{0:T(128)}) all-reduce(f32[]{:T(128)} %get-tuple-element.31, f32[2]{0:T(128)S(1)} %get-tuple-element.32), channel_id=1, replica_groups=mesh['gx_0'=4,'gx_1'=2,'gy_0'=4,'gy_1'=4] {'gy_0'}, use_global_device_ids=true, to_apply=%region_24.25 | all-reduce | flops 3 | bytes 24 | tf_op jit(solution)/shard_map/psum | solution.py:35
  198.7 6.6 %all-reduce.16 = (f32[]{:T(128)}, f32[2]{0:T(128)S(1)}) all-reduce(f32[]{:T(128)} %get-tuple-element.19, f32[2]{0:T(128)} %get-tuple-element.20), channel_id=1, replica_groups=mesh['gx_0'=4,'gx_1'=2,'gy_0'=4,'gy_1'=4] {'gy_1'}, use_global_device_ids=true, to_apply=%region_25.26 | all-reduce | flops 3 | bytes 24 | tf_op jit(solution)/shard_map/psum | solution.py:35
  207.8 5.0 %subtract_divide_fusion = f32[32,32,512]{2,1,0:T(8,128)S(1)} fusion(f32[32,32,512]{2,1,0:T(8,128)} %copy-done.2, f32[32,32,512]{2,1,0:T(8,128)} %get-tuple-element.35, f32[]{:T(128)S(6)} %sqrt.24, f32[]{:T(128)} %bitcast.6, f32[]{:T(128)} %bitcast.5, f32[32,32,512]{2,1,0:T(8,128)} %get-tuple-element.38, f32[]{:T(128)S(6)} %sqrt.21), kind=kLoop, calls=%fused_computation.137 | loop fusion | flops 3145728 | bytes 8388624 | tf_op jit(solution)/shard_map/div | solution.py:117
  212.8 0.9 fusion.76
  214.8 4.0 %collective-permute-start.18 = (f32[32,1,512]{2,1,0:T(1,128)}, f32[32,1,512]{2,1,0:T(1,128)}, u32[]{:S(2)}, u32[]{:S(2)}) collective-permute-start(f32[32,1,512]{2,1,0:T(1,128)} %get-tuple-element.41), channel_id=1, source_target_pairs={{0,1},{1,2},{2,3},{3,4},{4,5},{5,6},{6,7},{7,8},{8,9},{9,10},{10,1... | collective-permute-start | bytes 196616 | tf_op jit(solution)/shard_map/ppermute | solution.py:21
  218.8 1.3 collective-permute-start.19
  220.0 6.0 %collective-permute-start.16 = (f32[1,32,512]{2,1,0:T(8,128)}, f32[1,32,512]{2,1,0:T(8,128)}, u32[]{:S(2)}, u32[]{:S(2)}) collective-permute-start(f32[1,32,512]{2,1,0:T(8,128)} %get-tuple-element.39), channel_id=1, source_target_pairs={{0,16},{16,32},{32,48},{48,64},{64,80},{80,96},{96,112},{1,17},{17... | collective-permute-start | bytes 196616 | tf_op jit(solution)/shard_map/ppermute | solution.py:21
  226.0 2.5 collective-permute-start.17
  233.3 0.9 pad.59
  234.2 0.9 pad.60
  235.2 4.8 %select_maximum_fusion = f32[34,34,514]{2,1,0:T(8,128)S(1)} fusion(f32[34,1,512]{2,1,0:T(1,128)S(1)} %pad.60, f32[34,1,512]{2,1,0:T(1,128)S(1)} %pad.59, f32[1,32,512]{2,1,0:T(8,128)} %collective-permute-done.17, f32[32,32,512]{2,1,0:T(8,128)} %copy-done.10, f32[1,32,512]{2,1,0:T(8,128)} %collective-permute-done.16), kind=kLoop, calls=%fused_computation.2 | loop fusion | flops 7130208 | bytes 4744224 | tf_op jit(solution)/shard_map/concatenate | solution.py:28
  240.1 11.1 %multiply_reduce_fusion = (f32[]{:T(128)}, f32[]{:T(128)}, f32[]{:T(128)}, f32[]{:T(128)}) fusion(f32[32,32,512]{2,1,0:T(8,128)} %copy-done.10, f32[32,32,512]{2,1,0:T(8,128)S(1)} %copy-done.3, f32[34,34,514]{2,1,0:T(8,128)S(1)} %select_maximum_fusion, f32[32,32,512]{2,1,0:T(8,128)} %param.5, f32[34,34,514]{2,1,0:T(8,128)S(1)} %select_maximum_fusion.14, ...), kind=kLoop, calls=%fused_computation.133 | loop fusion | flops 26214400 | bytes 19546132 | tf_op jit(solution)/shard_map/reduce_sum | solution.py:109
  251.2 1.9 pad_maximum_fusion.33
  253.0 6.8 %all-reduce.21 = (f32[3]{0:T(128)S(1)}, f32[]{:T(128)}) all-reduce(f32[3]{0:T(128)S(1)} %pad_maximum_fusion.33, f32[]{:T(128)} %get-tuple-element.2), channel_id=1, replica_groups=mesh['gx_0'=4,'gx_1'=2,'gy_0'=4,'gy_1'=4] {'gx_0'}, use_global_device_ids=true, to_apply=%region_30.31 | all-reduce | flops 4 | bytes 32 | tf_op jit(solution)/shard_map/psum | solution.py:35
  259.8 5.9 %all-reduce.24 = (f32[3]{0:T(128)S(1)}, f32[]{:T(128)}) all-reduce(f32[3]{0:T(128)S(1)} %get-tuple-element.23, f32[]{:T(128)} %get-tuple-element.24), channel_id=1, replica_groups=mesh['gx_0'=4,'gx_1'=2,'gy_0'=4,'gy_1'=4] {'gx_1'}, use_global_device_ids=true, to_apply=%region_31.32 | all-reduce | flops 4 | bytes 32 | tf_op jit(solution)/shard_map/psum | solution.py:35
  265.7 9.0 %all-reduce.18 = (f32[3]{0:T(128)S(1)}, f32[]{:T(128)}) all-reduce(f32[3]{0:T(128)S(1)} %get-tuple-element.29, f32[]{:T(128)} %get-tuple-element.30), channel_id=1, replica_groups=mesh['gx_0'=4,'gx_1'=2,'gy_0'=4,'gy_1'=4] {'gy_0'}, use_global_device_ids=true, to_apply=%region_32.33 | all-reduce | flops 4 | bytes 32 | tf_op jit(solution)/shard_map/psum | solution.py:35
  274.7 6.6 %all-reduce.15 = (f32[3]{0:T(128)S(1)}, f32[]{:T(128)}) all-reduce(f32[3]{0:T(128)S(1)} %get-tuple-element.17, f32[]{:T(128)} %get-tuple-element.18), channel_id=1, replica_groups=mesh['gx_0'=4,'gx_1'=2,'gy_0'=4,'gy_1'=4] {'gy_1'}, use_global_device_ids=true, to_apply=%region_33.34 | all-reduce | flops 4 | bytes 32 | tf_op jit(solution)/shard_map/psum | solution.py:35
  281.3 0.7 multiply_reduce_fusion.10
  288.0 6.0 %multiply_add_fusion = f32[32,32,512]{2,1,0:T(8,128)} fusion(f32[32,32,512]{2,1,0:T(8,128)} %copy-done.10, f32[32,32,512]{2,1,0:T(8,128)} %copy-done.2, f32[32,32,512]{2,1,0:T(8,128)} %param.4, f32[]{:T(128)S(6)} %div.56, f32[]{:T(128)S(6)} %div.57, f32[]{:T(128)S(6)} %div.58, f32[32,32,512]{2,1,0:T(8,128)} %get-tuple-element.38, f32[]{:T(128)S(6)} %sqrt.21), kind=kLoop, calls=%fused_computation.132 | loop fusion | flops 3670016 | bytes 10485776 | tf_op jit(solution)/shard_map/add | solution.py:121
  (85 shorter events, 4.0 us)
Async XLA Ops:
  1.5 18.8 %collective-permute-start = (f32[1,32,512]{2,1,0:T(8,128)S(1)}, f32[1,32,512]{2,1,0:T(8,128)S(1)}, u32[]{:S(2)}, u32[]{:S(2)}) collective-permute-start(f32[1,32,512]{2,1,0:T(8,128)S(1)} %get-tuple-element.54), channel_id=1, source_target_pairs={{0,16},{16,32},{32,48},{48,64},{64,80},{80,96},{96,112},{1,17},{17... | collective-permute-start | bytes 196616 | tf_op jit(solution)/shard_map/ppermute | solution.py:21
  6.1 23.7 %collective-permute-start.2 = (f32[1,32,512]{2,1,0:T(8,128)S(1)}, f32[1,32,512]{2,1,0:T(8,128)S(1)}, u32[]{:S(2)}, u32[]{:S(2)}) collective-permute-start(f32[1,32,512]{2,1,0:T(8,128)S(1)} %get-tuple-element.53), channel_id=1, source_target_pairs={{16,0},{32,16},{48,32},{64,48},{80,64},{96,80},{112,96},{17,1},{33... | collective-permute-start | bytes 196616 | tf_op jit(solution)/shard_map/ppermute | solution.py:22
  9.4 14.8 %collective-permute-start.4 = (f32[32,1,512]{2,1,0:T(1,128)S(1)}, f32[32,1,512]{2,1,0:T(1,128)S(1)}, u32[]{:S(2)}, u32[]{:S(2)}) collective-permute-start(f32[32,1,512]{2,1,0:T(1,128)S(1)} %get-tuple-element.51), channel_id=1, source_target_pairs={{0,1},{1,2},{2,3},{3,4},{4,5},{5,6},{6,7},{7,8},{8,9},{9,10},{10,1... | collective-permute-start | bytes 196616 | tf_op jit(solution)/shard_map/ppermute | solution.py:21
  12.9 15.5 %collective-permute-start.6 = (f32[32,1,512]{2,1,0:T(1,128)S(1)}, f32[32,1,512]{2,1,0:T(1,128)S(1)}, u32[]{:S(2)}, u32[]{:S(2)}) collective-permute-start(f32[32,1,512]{2,1,0:T(1,128)S(1)} %get-tuple-element.52), channel_id=1, source_target_pairs={{1,0},{2,1},{3,2},{4,3},{5,4},{6,5},{7,6},{8,7},{9,8},{10,9},{11,1... | collective-permute-start | bytes 196616 | tf_op jit(solution)/shard_map/ppermute | solution.py:22
  15.1 16.4 %collective-permute-start.1 = (f32[1,32,512]{2,1,0:T(8,128)S(1)}, f32[1,32,512]{2,1,0:T(8,128)S(1)}, u32[]{:S(2)}, u32[]{:S(2)}) collective-permute-start(f32[1,32,512]{2,1,0:T(8,128)S(1)} %get-tuple-element.58), channel_id=1, source_target_pairs={{0,16},{16,32},{32,48},{48,64},{64,80},{80,96},{96,112},{1,17},{17... | collective-permute-start | bytes 196616 | tf_op jit(solution)/shard_map/ppermute | solution.py:21
  20.4 15.0 %copy-start.16 = (f32[1,32,512]{2,1,0:T(8,128)}, f32[1,32,512]{2,1,0:T(8,128)S(1)}, u32[]{:S(2)}) copy-start(f32[1,32,512]{2,1,0:T(8,128)S(1)} %collective-permute-done) | copy-start | bytes 196612
  20.4 13.3 %collective-permute-start.3 = (f32[1,32,512]{2,1,0:T(8,128)S(1)}, f32[1,32,512]{2,1,0:T(8,128)S(1)}, u32[]{:S(2)}, u32[]{:S(2)}) collective-permute-start(f32[1,32,512]{2,1,0:T(8,128)S(1)} %get-tuple-element.57), channel_id=1, source_target_pairs={{16,0},{32,16},{48,32},{64,48},{80,64},{96,80},{112,96},{17,1},{33... | collective-permute-start | bytes 196616 | tf_op jit(solution)/shard_map/ppermute | solution.py:22
  24.1 8.3 %collective-permute-start.5 = (f32[32,1,512]{2,1,0:T(1,128)S(1)}, f32[32,1,512]{2,1,0:T(1,128)S(1)}, u32[]{:S(2)}, u32[]{:S(2)}) collective-permute-start(f32[32,1,512]{2,1,0:T(1,128)S(1)} %get-tuple-element.55), channel_id=1, source_target_pairs={{0,1},{1,2},{2,3},{3,4},{4,5},{5,6},{6,7},{7,8},{8,9},{9,10},{10,1... | collective-permute-start | bytes 196616 | tf_op jit(solution)/shard_map/ppermute | solution.py:21
  28.5 5.2 %collective-permute-start.7 = (f32[32,1,512]{2,1,0:T(1,128)S(1)}, f32[32,1,512]{2,1,0:T(1,128)S(1)}, u32[]{:S(2)}, u32[]{:S(2)}) collective-permute-start(f32[32,1,512]{2,1,0:T(1,128)S(1)} %get-tuple-element.56), channel_id=1, source_target_pairs={{1,0},{2,1},{3,2},{4,3},{5,4},{6,5},{7,6},{8,7},{9,8},{10,9},{11,1... | collective-permute-start | bytes 196616 | tf_op jit(solution)/shard_map/ppermute | solution.py:22
  29.8 5.5 %copy-start.12 = (f32[34,1,512]{2,1,0:T(1,128)}, f32[34,1,512]{2,1,0:T(1,128)S(1)}, u32[]{:S(2)}) copy-start(f32[34,1,512]{2,1,0:T(1,128)S(1)} %pad.49) | copy-start | bytes 208900
  29.8 5.5 %copy-start.20 = (f32[1,32,512]{2,1,0:T(8,128)}, f32[1,32,512]{2,1,0:T(8,128)S(1)}, u32[]{:S(2)}) copy-start(f32[1,32,512]{2,1,0:T(8,128)S(1)} %collective-permute-done.2) | copy-start | bytes 196612
  29.9 5.5 %copy-start.4 = (f32[34,32,512]{2,1,0:T(8,128)}, f32[34,32,512]{2,1,0:T(8,128)S(1)}, u32[]{:S(2)}) copy-start(f32[34,32,512]{2,1,0:T(8,128)S(1)} %constant_dynamic-update-slice_fusion) | copy-start | bytes 6684676
  29.9 2.4 copy-start.11
  33.7 1.6 copy-start.7
  83.5 10.4 %collective-permute-start.10 = (f32[32,1,512]{2,1,0:T(1,128)S(1)}, f32[32,1,512]{2,1,0:T(1,128)S(1)}, u32[]{:S(2)}, u32[]{:S(2)}) collective-permute-start(f32[32,1,512]{2,1,0:T(1,128)S(1)} %get-tuple-element.49), channel_id=1, source_target_pairs={{0,1},{1,2},{2,3},{3,4},{4,5},{5,6},{6,7},{7,8},{8,9},{9,10},{10,1... | collective-permute-start | bytes 196616 | tf_op jit(solution)/shard_map/ppermute | solution.py:21
  84.8 9.2 %collective-permute-start.11 = (f32[32,1,512]{2,1,0:T(1,128)S(1)}, f32[32,1,512]{2,1,0:T(1,128)S(1)}, u32[]{:S(2)}, u32[]{:S(2)}) collective-permute-start(f32[32,1,512]{2,1,0:T(1,128)S(1)} %get-tuple-element.50), channel_id=1, source_target_pairs={{1,0},{2,1},{3,2},{4,3},{5,4},{6,5},{7,6},{8,7},{9,8},{10,9},{11,1... | collective-permute-start | bytes 196616 | tf_op jit(solution)/shard_map/ppermute | solution.py:22
  86.1 8.0 %collective-permute-start.8 = (f32[1,32,512]{2,1,0:T(8,128)S(1)}, f32[1,32,512]{2,1,0:T(8,128)S(1)}, u32[]{:S(2)}, u32[]{:S(2)}) collective-permute-start(f32[1,32,512]{2,1,0:T(8,128)S(1)} %get-tuple-element.47), channel_id=1, source_target_pairs={{0,16},{16,32},{32,48},{48,64},{64,80},{80,96},{96,112},{1,17},{17... | collective-permute-start | bytes 196616 | tf_op jit(solution)/shard_map/ppermute | solution.py:21
  91.7 5.6 %collective-permute-start.9 = (f32[1,32,512]{2,1,0:T(8,128)S(1)}, f32[1,32,512]{2,1,0:T(8,128)S(1)}, u32[]{:S(2)}, u32[]{:S(2)}) collective-permute-start(f32[1,32,512]{2,1,0:T(8,128)S(1)} %get-tuple-element.48), channel_id=1, source_target_pairs={{16,0},{32,16},{48,32},{64,48},{80,64},{96,80},{112,96},{17,1},{33... | collective-permute-start | bytes 196616 | tf_op jit(solution)/shard_map/ppermute | solution.py:22
  94.0 6.6 %copy-start.5 = (f32[34,32,512]{2,1,0:T(8,128)S(1)}, f32[34,32,512]{2,1,0:T(8,128)}, u32[]{:S(2)}) copy-start(f32[34,32,512]{2,1,0:T(8,128)} %copy-done.4) | copy-start | bytes 6684676
  94.0 6.6 %copy-start.8 = (f32[32,32,512]{2,1,0:T(8,128)S(1)}, f32[32,32,512]{2,1,0:T(8,128)}, u32[]{:S(2)}) copy-start(f32[32,32,512]{2,1,0:T(8,128)} %param.5) | copy-start | bytes 6291460
  94.1 6.6 %copy-start.13 = (f32[34,1,512]{2,1,0:T(1,128)S(1)}, f32[34,1,512]{2,1,0:T(1,128)}, u32[]{:S(2)}) copy-start(f32[34,1,512]{2,1,0:T(1,128)} %copy-done.12) | copy-start | bytes 208900
  94.1 6.6 %copy-start.17 = (f32[1,32,512]{2,1,0:T(8,128)S(1)}, f32[1,32,512]{2,1,0:T(8,128)}, u32[]{:S(2)}) copy-start(f32[1,32,512]{2,1,0:T(8,128)} %copy-done.16) | copy-start | bytes 196612
  94.1 6.6 %copy-start.21 = (f32[1,32,512]{2,1,0:T(8,128)S(1)}, f32[1,32,512]{2,1,0:T(8,128)}, u32[]{:S(2)}) copy-start(f32[1,32,512]{2,1,0:T(8,128)} %copy-done.20) | copy-start | bytes 196612
  145.4 20.6 %copy-start.2 = (f32[32,32,512]{2,1,0:T(8,128)}, f32[32,32,512]{2,1,0:T(8,128)S(1)}, u32[]{:S(2)}) copy-start(f32[32,32,512]{2,1,0:T(8,128)S(1)} %subtract_divide_fusion.1) | copy-start | bytes 6291460
  145.4 20.6 %copy-start.9 = (f32[32,32,512]{2,1,0:T(8,128)S(1)}, f32[32,32,512]{2,1,0:T(8,128)}, u32[]{:S(2)}) copy-start(f32[32,32,512]{2,1,0:T(8,128)} %param.5) | copy-start | bytes 6291460
  145.5 13.5 %collective-permute-start.14 = (f32[32,1,512]{2,1,0:T(1,128)S(1)}, f32[32,1,512]{2,1,0:T(1,128)S(1)}, u32[]{:S(2)}, u32[]{:S(2)}) collective-permute-start(f32[32,1,512]{2,1,0:T(1,128)S(1)} %get-tuple-element.45), channel_id=1, source_target_pairs={{0,1},{1,2},{2,3},{3,4},{4,5},{5,6},{6,7},{7,8},{8,9},{9,10},{10,1... | collective-permute-start | bytes 196616 | tf_op jit(solution)/shard_map/ppermute | solution.py:21
  149.2 9.9 %collective-permute-start.15 = (f32[32,1,512]{2,1,0:T(1,128)S(1)}, f32[32,1,512]{2,1,0:T(1,128)S(1)}, u32[]{:S(2)}, u32[]{:S(2)}) collective-permute-start(f32[32,1,512]{2,1,0:T(1,128)S(1)} %get-tuple-element.46), channel_id=1, source_target_pairs={{1,0},{2,1},{3,2},{4,3},{5,4},{6,5},{7,6},{8,7},{9,8},{10,9},{11,1... | collective-permute-start | bytes 196616 | tf_op jit(solution)/shard_map/ppermute | solution.py:22
  150.5 8.8 %collective-permute-start.12 = (f32[1,32,512]{2,1,0:T(8,128)S(1)}, f32[1,32,512]{2,1,0:T(8,128)S(1)}, u32[]{:S(2)}, u32[]{:S(2)}) collective-permute-start(f32[1,32,512]{2,1,0:T(8,128)S(1)} %get-tuple-element.43), channel_id=1, source_target_pairs={{0,16},{16,32},{32,48},{48,64},{64,80},{80,96},{96,112},{1,17},{17... | collective-permute-start | bytes 196616 | tf_op jit(solution)/shard_map/ppermute | solution.py:21
  157.1 5.6 %collective-permute-start.13 = (f32[1,32,512]{2,1,0:T(8,128)S(1)}, f32[1,32,512]{2,1,0:T(8,128)S(1)}, u32[]{:S(2)}, u32[]{:S(2)}) collective-permute-start(f32[1,32,512]{2,1,0:T(8,128)S(1)} %get-tuple-element.44), channel_id=1, source_target_pairs={{16,0},{32,16},{48,32},{64,48},{80,64},{96,80},{112,96},{17,1},{33... | collective-permute-start | bytes 196616 | tf_op jit(solution)/shard_map/ppermute | solution.py:22
  159.2 6.8 %copy-start = (f32[32,32,512]{2,1,0:T(8,128)S(1)}, f32[32,32,512]{2,1,0:T(8,128)}, u32[]{:S(2)}) copy-start(f32[32,32,512]{2,1,0:T(8,128)} %get-tuple-element.38) | copy-start | bytes 6291460
  159.2 6.8 %copy-start.6 = (f32[34,32,512]{2,1,0:T(8,128)S(1)}, f32[34,32,512]{2,1,0:T(8,128)}, u32[]{:S(2)}) copy-start(f32[34,32,512]{2,1,0:T(8,128)} %copy-done.4) | copy-start | bytes 6684676
  159.2 6.8 %copy-start.14 = (f32[34,1,512]{2,1,0:T(1,128)S(1)}, f32[34,1,512]{2,1,0:T(1,128)}, u32[]{:S(2)}) copy-start(f32[34,1,512]{2,1,0:T(1,128)} %copy-done.12) | copy-start | bytes 208900
  159.2 6.8 %copy-start.18 = (f32[1,32,512]{2,1,0:T(8,128)S(1)}, f32[1,32,512]{2,1,0:T(8,128)}, u32[]{:S(2)}) copy-start(f32[1,32,512]{2,1,0:T(8,128)} %copy-done.16) | copy-start | bytes 196612
  159.2 6.8 %copy-start.22 = (f32[1,32,512]{2,1,0:T(8,128)S(1)}, f32[1,32,512]{2,1,0:T(8,128)}, u32[]{:S(2)}) copy-start(f32[1,32,512]{2,1,0:T(8,128)} %copy-done.20) | copy-start | bytes 196612
  212.7 1.4 copy-start.10
  214.8 18.5 %collective-permute-start.18 = (f32[32,1,512]{2,1,0:T(1,128)}, f32[32,1,512]{2,1,0:T(1,128)}, u32[]{:S(2)}, u32[]{:S(2)}) collective-permute-start(f32[32,1,512]{2,1,0:T(1,128)} %get-tuple-element.41), channel_id=1, source_target_pairs={{0,1},{1,2},{2,3},{3,4},{4,5},{5,6},{6,7},{7,8},{8,9},{9,10},{10,1... | collective-permute-start | bytes 196616 | tf_op jit(solution)/shard_map/ppermute | solution.py:21
  218.8 15.5 %collective-permute-start.19 = (f32[32,1,512]{2,1,0:T(1,128)}, f32[32,1,512]{2,1,0:T(1,128)}, u32[]{:S(2)}, u32[]{:S(2)}) collective-permute-start(f32[32,1,512]{2,1,0:T(1,128)} %get-tuple-element.42), channel_id=1, source_target_pairs={{1,0},{2,1},{3,2},{4,3},{5,4},{6,5},{7,6},{8,7},{9,8},{10,9},{11,1... | collective-permute-start | bytes 196616 | tf_op jit(solution)/shard_map/ppermute | solution.py:22
  220.0 15.1 %collective-permute-start.16 = (f32[1,32,512]{2,1,0:T(8,128)}, f32[1,32,512]{2,1,0:T(8,128)}, u32[]{:S(2)}, u32[]{:S(2)}) collective-permute-start(f32[1,32,512]{2,1,0:T(8,128)} %get-tuple-element.39), channel_id=1, source_target_pairs={{0,16},{16,32},{32,48},{48,64},{64,80},{80,96},{96,112},{1,17},{17... | collective-permute-start | bytes 196616 | tf_op jit(solution)/shard_map/ppermute | solution.py:21
  226.0 9.1 %collective-permute-start.17 = (f32[1,32,512]{2,1,0:T(8,128)}, f32[1,32,512]{2,1,0:T(8,128)}, u32[]{:S(2)}, u32[]{:S(2)}) collective-permute-start(f32[1,32,512]{2,1,0:T(8,128)} %get-tuple-element.40), channel_id=1, source_target_pairs={{16,0},{32,16},{48,32},{64,48},{80,64},{96,80},{112,96},{17,1},{33... | collective-permute-start | bytes 196616 | tf_op jit(solution)/shard_map/ppermute | solution.py:22
  235.1 4.9 %copy-start.1 = (f32[32,32,512]{2,1,0:T(8,128)S(1)}, f32[32,32,512]{2,1,0:T(8,128)}, u32[]{:S(2)}) copy-start(f32[32,32,512]{2,1,0:T(8,128)} %get-tuple-element.38) | copy-start | bytes 6291460
  235.1 4.9 %copy-start.3 = (f32[32,32,512]{2,1,0:T(8,128)S(1)}, f32[32,32,512]{2,1,0:T(8,128)}, u32[]{:S(2)}) copy-start(f32[32,32,512]{2,1,0:T(8,128)} %copy-done.2) | copy-start | bytes 6291460
  235.1 4.9 %copy-start.15 = (f32[34,1,512]{2,1,0:T(1,128)S(1)}, f32[34,1,512]{2,1,0:T(1,128)}, u32[]{:S(2)}) copy-start(f32[34,1,512]{2,1,0:T(1,128)} %copy-done.12) | copy-start | bytes 208900
  235.1 4.9 %copy-start.19 = (f32[1,32,512]{2,1,0:T(8,128)S(1)}, f32[1,32,512]{2,1,0:T(8,128)}, u32[]{:S(2)}) copy-start(f32[1,32,512]{2,1,0:T(8,128)} %copy-done.16) | copy-start | bytes 196612
  235.2 4.9 %copy-start.23 = (f32[1,32,512]{2,1,0:T(8,128)S(1)}, f32[1,32,512]{2,1,0:T(8,128)}, u32[]{:S(2)}) copy-start(f32[1,32,512]{2,1,0:T(8,128)} %copy-done.20) | copy-start | bytes 196612
where the time goes:
time: 300 us; the launch traced here: 295 us
  blocking collectives  124 us (41%)
  other arithmetic  73.3 us (24%)
  starting transfers between devices  60.3 us (20%)
  between operations  16.6 us (6%)
  local copies, waits for them, and re-layouts  13 us (4%)
  waiting for transfers between devices  7.86 us (3%)
    psum x16, blocking collectives, over_axes(): x = lax.psum(x, axis)  124 us
    ppermute x10, starting transfers between devices, with_halo(): lax.ppermute(last, axis, up)  43.5 us
    reduce_sum x2, other arithmetic, local(): jnp.sum(vector * basis[earlier])  18.3 us
    ppermute x10, starting transfers between devices, with_halo(): lax.ppermute(initial, axis, [(b, a) for a, b in up])  16.8 us
    concatenate x5, other arithmetic, with_halo(): jnp.concatenate([jnp.pad(low, around), x, jnp.pad(high, around)], axis=dim)  14.6 us
    reduce_sum x1, other arithmetic, local(): jnp.sum(vector * vector)  11.1 us
    reduce_sum x1, other arithmetic, global_norm(): return jnp.sqrt(over_axes(jnp.sum(vector * vector), GX_GY))  8.7 us
    div x2, other arithmetic, local(): basis.append(vector / length)  8.35 us
  transfers between devices with their start and end apart: 20, of which 3 were waited for; matrix products, arithmetic and copies ran while one was open for 3% of the time, Pallas kernels for 0%

commit v1 on v0

v1 whole, which is shorter than its diff:
```python
import functools

import jax
import jax.numpy as jnp
from jax import lax
from jax.experimental import pallas as pl
from jax.experimental.pallas import tpu as pltpu
from jax.sharding import PartitionSpec as P

MESH = pl.DeviceIdType.MESH
F32 = jnp.float32
SCALE = 64.0
HALF = 0.5 / SCALE
R0, R1 = 8, 136
PLANES, ROWS = 34, 144


def renorm(a, b):
    s = a + b
    return s, b - (s - a)


def two_sum(a, b):
    s = a + b
    t = s - a
    return s, (a - (s - t)) + (b - t)


def split(a):
    t = 4097.0 * a
    high = t - (t - a)
    return high, a - high


def two_prod(a, b):
    p = a * b
    (ah, al), (bh, bl) = split(a), split(b)
    return p, ((ah * bh - p) + ah * bl + al * bh) + al * bl


def add(a, b):
    s, e = two_sum(a[0], b[0])
    return renorm(s, e + (a[1] + b[1]))


def sub(a, b):
    return add(a, (-b[0], -b[1]))


def mul(a, b):
    p, e = two_prod(a[0], b[0])
    return renorm(p, e + (a[0] * b[1] + a[1] * b[0]))


def div(a, b):
    q = a[0] / b[0]
    p, e = two_prod(q, b[0])
    return renorm(q, (((a[0] - p) - e) + (a[1] - q * b[1])) / b[0])


def normal_equations(m):
    l21, l31 = div(m[3], m[2]), div(m[4], m[2])
    d2 = sub(m[4], mul(l21, m[3]))
    e2 = sub(m[5], mul(l21, m[4]))
    l32 = div(e2, d2)
    d3 = sub(sub(m[6], mul(l31, m[4])), mul(l32, e2))
    c1 = m[1]
    c2 = sub(m[2], mul(l21, c1))
    c3 = sub(sub(m[3], mul(l31, c1)), mul(l32, c2))
    q1, q2, q3 = div(c1, m[2]), div(c2, d2), div(c3, d3)
    y3 = q3
    y2 = sub(q2, mul(l32, y3))
    y1 = sub(sub(q1, mul(l21, y2)), mul(l31, y3))
    rest = sub(sub(sub(m[0], mul(c1, q1)), mul(c2, q2)), mul(c3, q3))
    return tuple(y[0] / SCALE for y in (y1, y2, y3)), rest[0]


def directions(gx, gy, ngx, ngy):
    return (
        ("gy", 1, gy < ngy - 1, gy > 0),
        ("gy", -1, gy > 0, gy < ngy - 1),
        ("gx", 1, gx < ngx - 1, gx > 0),
        ("gx", -1, gx > 0, gx < ngx - 1),
    )


def face(ref, axis, step):
    if axis == "gx":
        return ref.at[32 if step > 0 else 1, R0:R1, :]
    return ref.at[1:33, (R1 - 4 if step > 0 else R0) : (R1 if step > 0 else R0 + 4), :]


def halo(ref, axis, step):
    if axis == "gx":
        return ref.at[0 if step > 0 else 33, R0:R1, :]
    return ref.at[1:33, (R0 - 4 if step > 0 else R1) : (R0 if step > 0 else R1 + 4), :]


def kernel(
    ngx, ngy,
    rhs_hbm, x0_hbm, k_hbm, sol_ref, est_ref,
    kp, up, rp, v1, v2, rb, wx, wy, wzm, wzp, dg, row, gath,
    load_sem, send_sem, recv_sem, gsend, grecv, ready,
):
    gx, gy = lax.axis_index("gx"), lax.axis_index("gy")
    count = ngx * ngy
    loads = []
    for i, (src, dst) in enumerate(((k_hbm, kp), (x0_hbm, up))):
        view = dst.reshape(PLANES, ROWS // 4, 4, 128)
        for q in range(4):
            loads.append(
                pltpu.make_async_copy(
                    src.at[:, :, q * 128 : (q + 1) * 128], view.at[1:33, 2:34, q, :], load_sem.at[i, q]
                )
            )
    view = rb.reshape(32, 32, 4, 128)
    for q in range(4):
        loads.append(
            pltpu.make_async_copy(rhs_hbm.at[:, :, q * 128 : (q + 1) * 128], view.at[:, :, q, :], load_sem.at[2, q])
        )
    for copy in loads:
        copy.start()

    barrier = pltpu.get_barrier_semaphore()
    for d in range(1, ngx):
        pl.semaphore_signal(barrier, inc=1, device_id=(lax.rem(gx + d, ngx), gy), device_id_type=MESH)
    for d in range(1, ngy):
        pl.semaphore_signal(barrier, inc=1, device_id=(gx, lax.rem(gy + d, ngy)), device_id_type=MESH)

    dirs = directions(gx, gy, ngx, ngy)
    fields = (kp, up, rp, v1, v2)
    zplane = jnp.zeros((R1 - R0, 128), F32)
    zrow = jnp.zeros((4, 128), F32)

    @pl.when(gx == 0)
    def _():
        for f in fields:
            f[0, R0:R1, :] = zplane

    @pl.when(gx == ngx - 1)
    def _():
        for f in fields:
            f[33, R0:R1, :] = zplane

    for at, edge in ((R0 - 4, 0), (R1, ngy - 1)):

        @pl.when(gy == edge)
        def _():
            def fill(x, c):
                for f in fields:
                    f[x, at : at + 4, :] = zrow
                return c

            lax.fori_loop(1, 33, fill, 0)

    def exchange(e, f, axes=("gx", "gy")):
        for i, (axis, step, to, _) in enumerate(dirs):
            if axis in axes:

                @pl.when(to)
                def _():
                    me = gx if axis == "gx" else gy
                    pltpu.make_async_remote_copy(
                        src_ref=face(f, axis, step), dst_ref=halo(f, axis, step),
                        send_sem=send_sem.at[e, i], recv_sem=recv_sem.at[e, i],
                        device_id={axis: me + step}, device_id_type=MESH,
                    ).start()

    def descriptor(e, f, i):
        axis, step = dirs[i][:2]
        return pltpu.make_async_remote_copy(
            src_ref=face(f, axis, step), dst_ref=halo(f, axis, step),
            send_sem=send_sem.at[e, i], recv_sem=recv_sem.at[e, i],
            device_id={axis: gx if axis == "gx" else gy}, device_id_type=MESH,
        )

    def arrived(e, f, axes):
        for i, (axis, _, _, come) in enumerate(dirs):
            if axis in axes:

                @pl.when(come)
                def _():
                    descriptor(e, f, i).wait_recv()

    def sent(e, f):
        for i, (_, _, to, _) in enumerate(dirs):

            @pl.when(to)
            def _():
                descriptor(e, f, i).wait_send()

    for copy in loads[:4]:
        copy.wait()
    pl.semaphore_wait(barrier, ngx + ngy - 2)
    exchange(0, kp)
    for copy in loads[4:8]:
        copy.wait()
    exchange(1, up)
    for d in range(1, ngx):
        pl.semaphore_signal(ready, inc=1, device_id=(lax.rem(gx + d, ngx), gy), device_id_type=MESH)

    lane = lax.broadcasted_iota(jnp.int32, (8, 128), 1)
    zhi = lax.rem(lax.broadcasted_iota(jnp.int32, (8, 128), 0), 4)
    first_lane, last_lane = lane == 0, lane == 127
    z_first = jnp.logical_and(first_lane, zhi == 0)
    z_last = jnp.logical_and(last_lane, zhi == 3)

    def z_up(f, x, r, centre):
        return pltpu.roll(jnp.where(first_lane, f[x, r + 1 : r + 9, :], centre), 127, 1)

    def z_down(f, x, r, centre):
        return pltpu.roll(jnp.where(last_lane, f[x, r - 1 : r + 7, :], centre), 1, 1)

    def weights_x(i, chunks):
        for r in chunks:
            wx[i, r - R0 : r - R0 + 8, :] = HALF * (kp[i, r : r + 8, :] + kp[i + 1, r : r + 8, :])

    def weights_y(x, r, n=8):
        wy[x, r : r + n, :] = HALF * (kp[x, r : r + n, :] + kp[x, r + 4 : r + 4 + n, :])

    def weights_z(x, r):
        centre = kp[x, r : r + 8, :]
        above = jnp.where(first_lane, pltpu.roll(centre, 7, 0), centre)
        below = jnp.where(last_lane, pltpu.roll(centre, 1, 0), centre)
        up_w = HALF * (centre + jnp.where(z_last, 0.0, pltpu.roll(above, 127, 1)))
        down_w = HALF * (centre + jnp.where(z_first, 0.0, pltpu.roll(below, 1, 1)))
        dg[x, r - R0 : r - R0 + 8, :] = up_w + down_w
        wzp[x, r - R0 : r - R0 + 8, :] = jnp.where(z_last, 0.0, up_w)
        wzm[x, r - R0 : r - R0 + 8, :] = jnp.where(z_first, 0.0, down_w)

    def add_diagonal(x, r):
        q = r - R0
        dg[x, q : q + 8, :] = dg[x, q : q + 8, :] + (
            (wx[x - 1, q : q + 8, :] + wx[x, q : q + 8, :]) + (wy[x, r - 4 : r + 4, :] + wy[x, r : r + 8, :])
        )

    def apply(f, x, r):
        q = r - R0
        centre = f[x, r : r + 8, :]
        out = dg[x, q : q + 8, :] * centre
        out = out - wx[x - 1, q : q + 8, :] * f[x - 1, r : r + 8, :]
        out = out - wx[x, q : q + 8, :] * f[x + 1, r : r + 8, :]
        out = out - wy[x, r - 4 : r + 4, :] * f[x, r - 4 : r + 4, :]
        out = out - wy[x, r : r + 8, :] * f[x, r + 4 : r + 12, :]
        out = out - wzm[x, q : q + 8, :] * z_down(f, x, r, centre)
        out = out - wzp[x, q : q + 8, :] * z_up(f, x, r, centre)
        return centre, out

    inner = tuple(range(R0 + 8, R1 - 8, 8))
    whole = tuple(range(R0, R1, 8))
    ends = (R0, R1 - 8)

    def over(planes, body, carry):
        if isinstance(planes, range):
            return lax.fori_loop(planes.start, planes.stop, body, carry)
        for x in planes:
            carry = body(x, carry)
        return carry

    def residual(planes, chunks, acc):
        def body(x, acc):
            for r in chunks:
                _, out = apply(up, x, r)
                out = rb[x - 1, r - R0 : r - R0 + 8, :] - SCALE * out
                rp[x, r : r + 8, :] = out
                acc = acc + out * out
            return acc

        return over(planes, body, acc)

    def power(f, w, planes, chunks, acc):
        def body(x, acc):
            cross, square = acc
            for r in chunks:
                centre, out = apply(f, x, r)
                if w is not None:
                    w[x, r : r + 8, :] = out
                cross, square = cross + centre * out, square + out * out
            return cross, square

        return over(planes, body, acc)

    def body(x, c):
        weights_x(x, whole)
        for r in whole[:-1]:
            weights_y(x, r)
        weights_y(x, R1 - 8, 4)
        for r in whole:
            weights_z(x, r)
        for r in inner:
            add_diagonal(x, r)
        return c

    weights_x(1, whole)
    lax.fori_loop(2, 32, body, 0)
    for x in (1, 32):
        for r in whole[:-1]:
            weights_y(x, r)
        weights_y(x, R1 - 8, 4)
        for r in whole:
            weights_z(x, r)
    for copy in loads[8:]:
        copy.wait()
    zero = jnp.zeros((8, 128), F32)
    m0 = residual(range(2, 32), inner, zero)
    arrived(0, kp, ("gx",))
    weights_x(0, whole)
    weights_x(32, whole)
    for x in (1, 32):
        for r in inner:
            add_diagonal(x, r)
    arrived(1, up, ("gx",))
    m0 = residual((1, 32), inner, m0)
    arrived(0, kp, ("gy",))

    def body(x, c):
        weights_y(x, R0 - 4, 4)
        weights_y(x, R1 - 4, 4)
        for r in ends:
            add_diagonal(x, r)
        return c

    lax.fori_loop(1, 33, body, 0)
    arrived(1, up, ("gy",))
    m0 = residual(range(1, 33), ends, m0)

    moments = [m0]
    for e, (f, w) in enumerate(((rp, v1), (v1, v2), (v2, None)), start=2):
        exchange(e, f)
        acc = power(f, w, range(2, 32), inner, (zero, zero))
        arrived(e, f, ("gx",))
        acc = power(f, w, (1, 32), inner, acc)
        arrived(e, f, ("gy",))
        acc = power(f, w, range(1, 33), ends, acc)
        moments.extend(acc)

    sub = lax.broadcasted_iota(jnp.int32, (8, 128), 0)
    stacked = zero
    for k, m in enumerate(moments):
        stacked = jnp.where(sub == k, jnp.sum(m, axis=0, keepdims=True), stacked)
    sums = jnp.sum(stacked, axis=1, keepdims=True)
    own = jnp.sum(jnp.where(lane == sub, sums, 0.0), axis=0, keepdims=True)
    place = gx * ngy + gy
    row[...] = own
    gath[pl.ds(place, 1), :] = own
    pl.semaphore_wait(ready, ngx - 1)

    def send(d, c):
        pltpu.make_async_remote_copy(
            src_ref=row, dst_ref=gath.at[pl.ds(place, 1), :], send_sem=gsend, recv_sem=grecv,
            device_id=(lax.rem(gx + d // ngy, ngx), lax.rem(gy + lax.rem(d, ngy), ngy)), device_id_type=MESH,
        ).start()
        return c

    lax.fori_loop(1, count, send, 0)
    every = pltpu.make_async_remote_copy(
        src_ref=gath.at[0 : count - 1, :], dst_ref=gath.at[0 : count - 1, :], send_sem=gsend, recv_sem=grecv,
        device_id=(gx, gy), device_id_type=MESH,
    )
    every.wait_recv()
    table = gath[...]
    bound = 2.0 * jnp.sum(jnp.abs(table), axis=0, keepdims=True)
    upper = (table + bound) - bound
    high = jnp.sum(upper, axis=0, keepdims=True)
    low = jnp.sum(table - upper, axis=0, keepdims=True)
    lane1 = lax.broadcasted_iota(jnp.int32, (1, 128), 1)

    def pick(v, k):
        return jnp.sum(jnp.where(lane1 == k, v, 0.0), axis=1, keepdims=True)

    m = [renorm(pick(high, k), pick(low, k)) for k in range(7)]
    (y1, y2, y3), rest = normal_equations(m)
    est_ref[...] = jnp.broadcast_to(jnp.sqrt(jnp.maximum(rest, 0.0)), (1, 128))
    y1, y2, y3 = (jnp.broadcast_to(y, (8, 128)) for y in (y1, y2, y3))

    def body(x, c):
        for r in whole:
            s = slice(r, r + 8)
            sol_ref[x - 1, r - R0 : r - R0 + 8, :] = up[x, s, :] + (
                y1 * rp[x, s, :] + (y2 * v1[x, s, :] + y3 * v2[x, s, :])
            )
        return c

    lax.fori_loop(1, 33, body, 0)
    every.wait_send()
    for e, f in enumerate((kp, up, rp, v1, v2)):
        sent(e, f)


def local(ngx, ngy, right_side, start_guess, conductivity):
    field = pltpu.VMEM((PLANES, ROWS, 128), F32)
    block = pltpu.VMEM((32, 128, 128), F32)
    sem = pltpu.SemaphoreType
    sol, est = pl.pallas_call(
        functools.partial(kernel, ngx, ngy),
        out_shape=(jax.ShapeDtypeStruct((32, 128, 128), F32), jax.ShapeDtypeStruct((1, 128), F32)),
        in_specs=[pl.BlockSpec(memory_space=pl.ANY)] * 3,
        out_specs=(pl.BlockSpec(memory_space=pltpu.VMEM), pl.BlockSpec(memory_space=pltpu.VMEM)),
        scratch_shapes=[field] * 5 + [
            block,
            pltpu.VMEM((33, 128, 128), F32),
            pltpu.VMEM((33, ROWS, 128), F32),
            pltpu.VMEM((33, 128, 128), F32),
            pltpu.VMEM((33, 128, 128), F32),
            pltpu.VMEM((33, 128, 128), F32),
            pltpu.VMEM((1, 128), F32),
            pltpu.VMEM((ngx * ngy, 128), F32),
            sem.DMA((3, 4)), sem.DMA((5, 4)), sem.DMA((5, 4)), sem.DMA, sem.DMA, sem.REGULAR,
        ],
        compiler_params=pltpu.CompilerParams(
            collective_id=0, has_side_effects=True, vmem_limit_bytes=62 * 2**20
        ),
    )(right_side, start_guess, conductivity)
    return sol.reshape(32, 32, 512), est[0, 0]


def solution(mesh):
    return jax.shard_map(
        functools.partial(local, mesh.shape["gx"], mesh.shape["gy"]),
        mesh=mesh,
        in_specs=(P("gx", "gy", None),) * 3,
        out_specs=(P("gx", "gy", None), P()),
        check_vma=False,
    )
```

time: 300 us -> 54 us (0.18); the launches traced: 295 us -> 53.9 us
  blocking collectives: 124 us -> 0 us
  other arithmetic: 73.3 us -> 0 us
  starting transfers between devices: 60.3 us -> 0 us
  Pallas kernels: 0 us -> 49.4 us
  between operations: 16.6 us -> 1.81 us
  local copies, waits for them, and re-layouts: 13 us -> 2.73 us
  waiting for transfers between devices: 7.86 us -> 0 us
    psum x16 -> x0, blocking collectives: 124 us -> none  [over_axes(): x = lax.psum(x, axis)]
    ppermute x20 -> x0, starting transfers between devices: 60.3 us -> none  [the longest x10 43.5 us: with_halo(): lax.ppermute(last, axis, up)]
    pallas_call x0 -> x1, Pallas kernels: none -> 49.4 us  [local(): pl.pallas_call(functools.partial(kernel, ngx, ngy), out_shape=(jax.ShapeD...]
    reduce_sum x6 -> x0, other arithmetic: 39.4 us -> none  [the longest x2 18.3 us: local(): jnp.sum(vector * basis[earlier])]
    concatenate x5 -> x0, other arithmetic: 14.6 us -> none  [with_halo(): jnp.concatenate([jnp.pad(low, around), x, jnp.pad(high, around)], axis=dim)]
    div x3 -> x0, other arithmetic: 10.2 us -> none  [the longest x2 8.35 us: local(): basis.append(vector / length)]
    ppermute x20 -> x0, waiting for transfers between devices: 7.86 us -> none  [the longest x10 7.83 us: with_halo(): lax.ppermute(initial, axis, [(b, a) for a, b in up])]
    slice x12 -> x0, local copies, waits for them, and re-layouts: 7.46 us -> none  [the longest x8 4.43 us: with_halo(): last = lax.slice_in_dim(x, length - width, length, axis=dim)]
  transfers between devices with their start and end apart: 20 -> 0, of which waited for: 3 -> 0; matrix products, arithmetic and copies ran while one was open for 3% -> 0% of each run, Pallas kernels for 0% -> 0%
where the time goes in v1:
time: 54 us; the launch traced here: 53.9 us
  Pallas kernels  49.4 us (91%)
  local copies, waits for them, and re-layouts  2.73 us (5%)
  between operations  1.81 us (3%)
    pallas_call x1, Pallas kernels, local(): pl.pallas_call(functools.partial(kernel, ngx, ngy), out_shape=(jax.ShapeD...  49.4 us
    reshape x1, local copies, waits for them, and re-layouts, local(): return (sol.reshape(32, 32, 512), est[0, 0])  2.72 us

profile of v1, /device:TPU:1, one launch (start us, length us, event | category | flops | bytes accessed | tf_op | source)
XLA Modules:
  0.0 53.9 jit_solution(12166307334767745939)
XLA Ops:
  0.6 49.4 %shard_map.50 = (f32[32,128,128]{2,1,0:T(8,128)}, f32[1,128]{1,0:T(1,128)}) custom-call(f32[32,32,512]{2,1,0:T(8,128)} %rhs_hbm.1, f32[32,32,512]{2,1,0:T(8,128)} %x0_hbm.1, f32[32,32,512]{2,1,0:T(8,128)} %k_hbm.1), custom_call_target="tpu_custom_call" | custom-call | tf_op jit(solution)/shard_map/pallas_call | solution.py:394
  50.0 0.0 copy-start
  50.0 2.7 %reshape.7 = f32[32,32,512]{2,1,0:T(8,128)} reshape(f32[32,128,128]{2,1,0:T(8,128)} %get-tuple-element.4) | data formatting | bytes 4194304 | tf_op jit(solution)/shard_map/reshape | solution.py:414
  52.7 0.0 copy-done
Async XLA Ops:
  50.0 2.7 %copy-start = (f32[1,128]{1,0:T(1,128)S(1)}, f32[1,128]{1,0:T(1,128)}, u32[]{:S(2)}) copy-start(f32[1,128]{1,0:T(1,128)} %get-tuple-element.5) | copy-start | bytes 1540

commit v2 on v1

--- a/solution.py
+++ b/solution.py
@@ -82,6 +82,14 @@
         ("gx", 1, gx < ngx - 1, gx > 0),
         ("gx", -1, gx > 0, gx < ngx - 1),
     )
+
+
+def far_first(ngx, ngy):
+    def ring(d):
+        return min(d % 4, -d % 4)
+
+    offsets = [(dx, dy) for dx in range(ngx) for dy in range(ngy) if dx or dy]
+    return sorted(offsets, key=lambda o: -(ring(o[0] // 2) + ring(o[1] // 4) + ring(o[1] % 4)))
 
 
 def face(ref, axis, step):
@@ -189,13 +197,15 @@
             def _():
                 descriptor(e, f, i).wait_send()
 
-    for copy in loads[:4]:
-        copy.wait()
-    pl.semaphore_wait(barrier, ngx + ngy - 2)
-    exchange(0, kp)
-    for copy in loads[4:8]:
-        copy.wait()
-    exchange(1, up)
+    with jax.named_scope("load_k"):
+        for copy in loads[:4]:
+            copy.wait()
+    with jax.named_scope("barrier"):
+        pl.semaphore_wait(barrier, ngx + ngy - 2)
+        exchange(0, kp)
+        for copy in loads[4:8]:
+            copy.wait()
+        exchange(1, up)
     for d in range(1, ngx):
         pl.semaphore_signal(ready, inc=1, device_id=(lax.rem(gx + d, ngx), gy), device_id_type=MESH)
 
@@ -250,12 +260,19 @@
     whole = tuple(range(R0, R1, 8))
     ends = (R0, R1 - 8)
 
-    def over(planes, body, carry):
-        if isinstance(planes, range):
-            return lax.fori_loop(planes.start, planes.stop, body, carry)
-        for x in planes:
-            carry = body(x, carry)
-        return carry
+    def over(planes, body, carry, unroll=1):
+        if not isinstance(planes, range):
+            for x in planes:
+                carry = body(x, carry)
+            return carry
+        first, steps = planes.start, len(planes) // unroll
+
+        def several(i, carry):
+            for u in range(unroll):
+                carry = body(first + i * unroll + u, carry)
+            return carry
+
+        return lax.fori_loop(0, steps, several, carry)
 
     def residual(planes, chunks, acc):
         def body(x, acc):
@@ -266,7 +283,7 @@
                 acc = acc + out * out
             return acc
 
-        return over(planes, body, acc)
+        return over(planes, body, acc, max(2, 16 // len(chunks) // 2 * 2))
 
     def power(f, w, planes, chunks, acc):
         def body(x, acc):
@@ -278,7 +295,7 @@
                 cross, square = cross + centre * out, square + out * out
             return cross, square
 
-        return over(planes, body, acc)
+        return over(planes, body, acc, max(2, 16 // len(chunks) // 2 * 2))
 
     def body(x, c):
         weights_x(x, whole)
@@ -291,19 +308,22 @@
             add_diagonal(x, r)
         return c
 
-    weights_x(1, whole)
-    lax.fori_loop(2, 32, body, 0)
-    for x in (1, 32):
-        for r in whole[:-1]:
-            weights_y(x, r)
-        weights_y(x, R1 - 8, 4)
-        for r in whole:
-            weights_z(x, r)
-    for copy in loads[8:]:
-        copy.wait()
-    zero = jnp.zeros((8, 128), F32)
-    m0 = residual(range(2, 32), inner, zero)
-    arrived(0, kp, ("gx",))
+    with jax.named_scope("weights"):
+        weights_x(1, whole)
+        lax.fori_loop(2, 32, body, 0)
+        for x in (1, 32):
+            for r in whole[:-1]:
+                weights_y(x, r)
+            weights_y(x, R1 - 8, 4)
+            for r in whole:
+                weights_z(x, r)
+    with jax.named_scope("r_inner"):
+        for copy in loads[8:]:
+            copy.wait()
+        zero = jnp.zeros((8, 128), F32)
+        m0 = residual(range(2, 32), inner, zero)
+    with jax.named_scope("wait_k_x"):
+        arrived(0, kp, ("gx",))
     weights_x(0, whole)
     weights_x(32, whole)
     for x in (1, 32):
@@ -311,7 +331,8 @@
             add_diagonal(x, r)
     arrived(1, up, ("gx",))
     m0 = residual((1, 32), inner, m0)
-    arrived(0, kp, ("gy",))
+    with jax.named_scope("wait_k_y"):
+        arrived(0, kp, ("gy",))
 
     def body(x, c):
         weights_y(x, R0 - 4, 4)
@@ -320,58 +341,65 @@
             add_diagonal(x, r)
         return c
 
-    lax.fori_loop(1, 33, body, 0)
-    arrived(1, up, ("gy",))
-    m0 = residual(range(1, 33), ends, m0)
+    over(range(1, 33), body, 0, 4)
+    with jax.named_scope("wait_u_y_r_ring"):
+        arrived(1, up, ("gy",))
+        m0 = residual(range(1, 33), ends, m0)
 
     moments = [m0]
     for e, (f, w) in enumerate(((rp, v1), (v1, v2), (v2, None)), start=2):
         exchange(e, f)
-        acc = power(f, w, range(2, 32), inner, (zero, zero))
-        arrived(e, f, ("gx",))
-        acc = power(f, w, (1, 32), inner, acc)
-        arrived(e, f, ("gy",))
-        acc = power(f, w, range(1, 33), ends, acc)
+        with jax.named_scope("inner%d" % e):
+            acc = power(f, w, range(2, 32), inner, (zero, zero))
+        with jax.named_scope("waitx%d" % e):
+            arrived(e, f, ("gx",))
+        with jax.named_scope("ringx%d" % e):
+            acc = power(f, w, (1, 32), inner, acc)
+        with jax.named_scope("waity%d" % e):
+            arrived(e, f, ("gy",))
+        with jax.named_scope("ringy%d" % e):
+            acc = power(f, w, range(1, 33), ends, acc)
         moments.extend(acc)
 
-    sub = lax.broadcasted_iota(jnp.int32, (8, 128), 0)
-    stacked = zero
-    for k, m in enumerate(moments):
-        stacked = jnp.where(sub == k, jnp.sum(m, axis=0, keepdims=True), stacked)
-    sums = jnp.sum(stacked, axis=1, keepdims=True)
-    own = jnp.sum(jnp.where(lane == sub, sums, 0.0), axis=0, keepdims=True)
-    place = gx * ngy + gy
+    with jax.named_scope("moments"):
+        sub = lax.broadcasted_iota(jnp.int32, (8, 128), 0)
+        stacked = zero
+        for k, m in enumerate(moments):
+            stacked = jnp.where(sub == k, jnp.sum(m, axis=0, keepdims=True), stacked)
+        sums = jnp.sum(stacked, axis=1, keepdims=True)
+        own = jnp.sum(jnp.where(lane == sub, sums, 0.0), axis=0, keepdims=True)
+        place = gx * ngy + gy
     row[...] = own
     gath[pl.ds(place, 1), :] = own
     pl.semaphore_wait(ready, ngx - 1)
 
-    def send(d, c):
-        pltpu.make_async_remote_copy(
-            src_ref=row, dst_ref=gath.at[pl.ds(place, 1), :], send_sem=gsend, recv_sem=grecv,
-            device_id=(lax.rem(gx + d // ngy, ngx), lax.rem(gy + lax.rem(d, ngy), ngy)), device_id_type=MESH,
-        ).start()
-        return c
-
-    lax.fori_loop(1, count, send, 0)
+    with jax.named_scope("gsend"):
+        for dx, dy in far_first(ngx, ngy):
+            pltpu.make_async_remote_copy(
+                src_ref=row, dst_ref=gath.at[pl.ds(place, 1), :], send_sem=gsend, recv_sem=grecv,
+                device_id=(lax.rem(gx + dx, ngx), lax.rem(gy + dy, ngy)), device_id_type=MESH,
+            ).start()
     every = pltpu.make_async_remote_copy(
         src_ref=gath.at[0 : count - 1, :], dst_ref=gath.at[0 : count - 1, :], send_sem=gsend, recv_sem=grecv,
         device_id=(gx, gy), device_id_type=MESH,
     )
-    every.wait_recv()
-    table = gath[...]
-    bound = 2.0 * jnp.sum(jnp.abs(table), axis=0, keepdims=True)
-    upper = (table + bound) - bound
-    high = jnp.sum(upper, axis=0, keepdims=True)
-    low = jnp.sum(table - upper, axis=0, keepdims=True)
-    lane1 = lax.broadcasted_iota(jnp.int32, (1, 128), 1)
-
-    def pick(v, k):
-        return jnp.sum(jnp.where(lane1 == k, v, 0.0), axis=1, keepdims=True)
-
-    m = [renorm(pick(high, k), pick(low, k)) for k in range(7)]
-    (y1, y2, y3), rest = normal_equations(m)
-    est_ref[...] = jnp.broadcast_to(jnp.sqrt(jnp.maximum(rest, 0.0)), (1, 128))
-    y1, y2, y3 = (jnp.broadcast_to(y, (8, 128)) for y in (y1, y2, y3))
+    with jax.named_scope("gwait"):
+        every.wait_recv()
+    with jax.named_scope("solve"):
+        table = gath[...]
+        bound = 2.0 * jnp.sum(jnp.abs(table), axis=0, keepdims=True)
+        upper = (table + bound) - bound
+        high = jnp.sum(upper, axis=0, keepdims=True)
+        low = jnp.sum(table - upper, axis=0, keepdims=True)
+        lane1 = lax.broadcasted_iota(jnp.int32, (1, 128), 1)
+
+        def pick(v, k):
+            return jnp.sum(jnp.where(lane1 == k, v, 0.0), axis=1, keepdims=True)
+
+        m = [renorm(pick(high, k), pick(low, k)) for k in range(7)]
+        (y1, y2, y3), rest = normal_equations(m)
+        est_ref[...] = jnp.broadcast_to(jnp.sqrt(jnp.maximum(rest, 0.0)), (1, 128))
+        y1, y2, y3 = (jnp.broadcast_to(y, (8, 128)) for y in (y1, y2, y3))
 
     def body(x, c):
         for r in whole:
@@ -381,7 +409,8 @@
             )
         return c
 
-    lax.fori_loop(1, 33, body, 0)
+    with jax.named_scope("final"):
+        lax.fori_loop(1, 33, body, 0)
     every.wait_send()
     for e, f in enumerate((kp, up, rp, v1, v2)):
         sent(e, f)
@@ -394,7 +423,7 @@
     sol, est = pl.pallas_call(
         functools.partial(kernel, ngx, ngy),
         out_shape=(jax.ShapeDtypeStruct((32, 128, 128), F32), jax.ShapeDtypeStruct((1, 128), F32)),
-        in_specs=[pl.BlockSpec(memory_space=pl.ANY)] * 3,
+        in_specs=[pl.BlockSpec(memory_space=pltpu.HBM)] * 3,
         out_specs=(pl.BlockSpec(memory_space=pltpu.VMEM), pl.BlockSpec(memory_space=pltpu.VMEM)),
         scratch_shapes=[field] * 5 + [
             block,
@@ -408,7 +437,7 @@
             sem.DMA((3, 4)), sem.DMA((5, 4)), sem.DMA((5, 4)), sem.DMA, sem.DMA, sem.REGULAR,
         ],
         compiler_params=pltpu.CompilerParams(
-            collective_id=0, has_side_effects=True, vmem_limit_bytes=62 * 2**20
+            collective_id=0, has_side_effects=True, vmem_limit_bytes=int(50 * 2**20)
         ),
     )(right_side, start_guess, conductivity)
     return sol.reshape(32, 32, 512), est[0, 0]

time: 54 us -> 40.2 us (0.74)
  Pallas kernels: 49.4 us -> 36.8 us
  local copies, waits for them, and re-layouts: 2.73 us -> 1.49 us
    pallas_call x1, Pallas kernels: 49.4 us -> 36.8 us  [local(): pl.pallas_call(functools.partial(kernel, ngx, ngy), out_shape=(jax.ShapeD...]
    reshape x1, local copies, waits for them, and re-layouts: 2.72 us -> 1.49 us  [local(): return (sol.reshape(32, 32, 512), est[0, 0])]
where the time goes in v2:
time: 40.2 us; the launch traced here: 40.1 us
  Pallas kernels  36.8 us (92%)
  between operations  1.8 us (4%)
  local copies, waits for them, and re-layouts  1.49 us (4%)
    pallas_call x1, Pallas kernels, local(): pl.pallas_call(functools.partial(kernel, ngx, ngy), out_shape=(jax.ShapeD...  36.8 us
    reshape x1, local copies, waits for them, and re-layouts, local(): return (sol.reshape(32, 32, 512), est[0, 0])  1.49 us

profile of v2, /device:TPU:1, one launch (start us, length us, event | category | flops | bytes accessed | tf_op | source)
XLA Modules:
  0.0 40.1 jit_solution(7172203063688188021)
XLA Ops:
  0.6 36.8 %shard_map.50 = (f32[32,128,128]{2,1,0:T(8,128)S(1)}, f32[1,128]{1,0:T(1,128)S(1)}) custom-call(f32[32,32,512]{2,1,0:T(8,128)} %rhs_hbm.1, f32[32,32,512]{2,1,0:T(8,128)} %x0_hbm.1, f32[32,32,512]{2,1,0:T(8,128)} %k_hbm.1), custom_call_target="tpu_custom_call" | custom-call | tf_op jit(solution)/shard_map/pallas_call | solution.py:423
  37.5 1.5 %reshape.7 = f32[32,32,512]{2,1,0:T(8,128)} reshape(f32[32,128,128]{2,1,0:T(8,128)S(1)} %get-tuple-element.4) | data formatting | bytes 4194304 | tf_op jit(solution)/shard_map/reshape | solution.py:443

commit v3 on v2

v3 whole, which is shorter than its diff:
```python
import functools

import jax
import jax.numpy as jnp
from jax import lax
from jax.experimental import pallas as pl
from jax.experimental.pallas import tpu as pltpu
from jax.sharding import PartitionSpec as P

MESH = pl.DeviceIdType.MESH
F32 = jnp.float32
SCALE = 64.0
HALF = 0.5 / SCALE
X0, X1 = 2, 34
R0, R1 = 16, 144
PLANES, ROWS = 36, 160


def renorm(a, b):
    s = a + b
    return s, b - (s - a)


def two_sum(a, b):
    s = a + b
    t = s - a
    return s, (a - (s - t)) + (b - t)


def split(a):
    t = 4097.0 * a
    high = t - (t - a)
    return high, a - high


def two_prod(a, b):
    p = a * b
    (ah, al), (bh, bl) = split(a), split(b)
    return p, ((ah * bh - p) + ah * bl + al * bh) + al * bl


def add(a, b):
    s, e = two_sum(a[0], b[0])
    return renorm(s, e + (a[1] + b[1]))


def sub(a, b):
    return add(a, (-b[0], -b[1]))


def mul(a, b):
    p, e = two_prod(a[0], b[0])
    return renorm(p, e + (a[0] * b[1] + a[1] * b[0]))


def div(a, b):
    q = a[0] / b[0]
    p, e = two_prod(q, b[0])
    return renorm(q, (((a[0] - p) - e) + (a[1] - q * b[1])) / b[0])


def split_sum(v, axis):
    bound = 2.0 * jnp.sum(jnp.abs(v), axis=axis, keepdims=True)
    upper = (v + bound) - bound
    return jnp.sum(upper, axis=axis, keepdims=True), jnp.sum(v - upper, axis=axis, keepdims=True)


def normal_equations(m):
    l21, l31 = div(m[3], m[2]), div(m[4], m[2])
    d2 = sub(m[4], mul(l21, m[3]))
    e2 = sub(m[5], mul(l21, m[4]))
    l32 = div(e2, d2)
    d3 = sub(sub(m[6], mul(l31, m[4])), mul(l32, e2))
    c1 = m[1]
    c2 = sub(m[2], mul(l21, c1))
    c3 = sub(sub(m[3], mul(l31, c1)), mul(l32, c2))
    q1, q2, q3 = div(c1, m[2]), div(c2, d2), div(c3, d3)
    y3 = q3
    y2 = sub(q2, mul(l32, y3))
    y1 = sub(sub(q1, mul(l21, y2)), mul(l31, y3))
    rest = sub(sub(sub(m[0], mul(c1, q1)), mul(c2, q2)), mul(c3, q3))
    return tuple(y[0] / SCALE for y in (y1, y2, y3)), rest[0]


def directions(gx, gy, ngx, ngy):
    out = []
    for sx, sy in ((0, 1), (0, -1), (1, 0), (-1, 0), (1, 1), (1, -1), (-1, 1), (-1, -1)):
        to, come = [], []
        for step, at, n in ((sx, gx, ngx), (sy, gy, ngy)):
            if step:
                to.append(at < n - 1 if step > 0 else at > 0)
                come.append(at > 0 if step > 0 else at < n - 1)
        both = (lambda c: c[0]) if len(to) == 1 else (lambda c: jnp.logical_and(*c))
        out.append((sx, sy, both(to), both(come)))
    return out


def far_first(ngx, ngy):
    def ring(d):
        return min(d % 4, -d % 4)

    offsets = [(dx, dy) for dx in range(ngx) for dy in range(ngy) if dx or dy]
    return sorted(offsets, key=lambda o: -(ring(o[0] // 2) + ring(o[1] // 4) + ring(o[1] % 4)))


def extent(step, low, high, depth, outside):
    if step == 0:
        return slice(low, high)
    if outside:
        return slice(low - depth, low) if step > 0 else slice(high, high + depth)
    return slice(high - depth, high) if step > 0 else slice(low, low + depth)


def piece(ref, sx, sy, depth, outside):
    if sx and sy:
        depth = 1
    return ref.at[extent(sx, X0, X1, depth, outside), extent(sy, R0, R1, 4 * depth, outside), :]


def kernel(
    ngx, ngy,
    rhs_hbm, x0_hbm, k_hbm, sol_ref, est_ref,
    kp, up, rb, rp, v1, v2, wx, wy, wzm, wzp, dg, row, gath,
    load_sem, send_sem, recv_sem, gsend, grecv, ready,
):
    gx, gy = lax.axis_index("gx"), lax.axis_index("gy")
    count = ngx * ngy
    loads = []
    for i, (src, dst) in enumerate(((k_hbm, kp), (x0_hbm, up), (rhs_hbm, rb))):
        view = dst.reshape(PLANES, ROWS // 4, 4, 128)
        for q in range(4):
            loads.append(
                pltpu.make_async_copy(
                    src.at[:, :, q * 128 : (q + 1) * 128],
                    view.at[X0:X1, R0 // 4 : R1 // 4, q, :],
                    load_sem.at[i, q],
                )
            )
    for copy in loads:
        copy.start()

    barrier = pltpu.get_barrier_semaphore()
    greet = [(d, 0) for d in range(1, ngx)] + [(0, d) for d in range(1, ngy)]
    greet += [(1, 1), (1, ngy - 1), (ngx - 1, 1), (ngx - 1, ngy - 1)]
    for dx, dy in greet:
        pl.semaphore_signal(
            barrier, inc=1, device_id=(lax.rem(gx + dx, ngx), lax.rem(gy + dy, ngy)), device_id_type=MESH
        )

    dirs = directions(gx, gy, ngx, ngy)
    has_low_x, has_high_x, has_low_y, has_high_y = gx > 0, gx < ngx - 1, gy > 0, gy < ngy - 1
    fields = (kp, up, rp, v1, v2)
    zero = jnp.zeros((8, 128), F32)

    for at, inside in ((0, has_low_x), (X1, has_high_x)):

        @pl.when(jnp.logical_not(inside))
        def _():
            def fill(i, c):
                for f in fields:
                    for x in (at, at + 1):
                        f[x, pl.ds(pl.multiple_of(8 + 8 * i, 8), 8), :] = zero
                return c

            lax.fori_loop(0, 18, fill, 0)

    for at, inside in ((R0 - 8, has_low_y), (R1, has_high_y)):

        @pl.when(jnp.logical_not(inside))
        def _():
            def fill(x, c):
                for f in fields:
                    f[x, at : at + 8, :] = zero
                return c

            lax.fori_loop(0, PLANES, fill, 0)

    def copy_of(e, f, depth, i):
        sx, sy = dirs[i][:2]
        return pltpu.make_async_remote_copy(
            src_ref=piece(f, sx, sy, depth, False), dst_ref=piece(f, sx, sy, depth, True),
            send_sem=send_sem.at[e, i], recv_sem=recv_sem.at[e, i],
            device_id={"gx": lax.rem(gx + sx + ngx, ngx), "gy": lax.rem(gy + sy + ngy, ngy)},
            device_id_type=MESH,
        )

    def exchange(e, f, depth, which):
        for i in which:

            @pl.when(dirs[i][2])
            def _():
                copy_of(e, f, depth, i).start()

    def arrived(e, f, depth, which):
        for i in which:

            @pl.when(dirs[i][3])
            def _():
                copy_of(e, f, depth, i).wait_recv()

    def sent(e, f, depth, which):
        for i in which:

            @pl.when(dirs[i][2])
            def _():
                copy_of(e, f, depth, i).wait_send()

    along_y, along_x, corners = (0, 1), (2, 3), (4, 5, 6, 7)
    every_way = along_y + along_x + corners
    faces = along_y + along_x

    with jax.named_scope("load_k"):
        for copy in loads[:4]:
            copy.wait()
    with jax.named_scope("barrier"):
        pl.semaphore_wait(barrier, len(greet))
        exchange(0, kp, 2, every_way)
        for copy in loads[4:8]:
            copy.wait()
        exchange(1, up, 2, every_way)
        for copy in loads[8:]:
            copy.wait()
        exchange(2, rb, 1, faces)
        for d in range(1, ngx):
            pl.semaphore_signal(ready, inc=1, device_id=(lax.rem(gx + d, ngx), gy), device_id_type=MESH)

    lane = lax.broadcasted_iota(jnp.int32, (8, 128), 1)
    sub = lax.broadcasted_iota(jnp.int32, (8, 128), 0)
    zhi = lax.rem(sub, 4)
    first_lane, last_lane = lane == 0, lane == 127
    z_first = jnp.logical_and(first_lane, zhi == 0)
    z_last = jnp.logical_and(last_lane, zhi == 3)

    def z_up(f, x, r, centre):
        return pltpu.roll(jnp.where(first_lane, f[x, r + 1 : r + 9, :], centre), 127, 1)

    def z_down(f, x, r, centre):
        return pltpu.roll(jnp.where(last_lane, f[x, r - 1 : r + 7, :], centre), 1, 1)

    def weights_x(i, r):
        wx[i, r : r + 8, :] = HALF * (kp[i, r : r + 8, :] + kp[i + 1, r : r + 8, :])

    def weights_y(x, r, n=8):
        wy[x, r : r + n, :] = HALF * (kp[x, r : r + n, :] + kp[x, r + 4 : r + 4 + n, :])

    def weights_z(x, r):
        centre = kp[x, r : r + 8, :]
        above = jnp.where(first_lane, pltpu.roll(centre, 7, 0), centre)
        below = jnp.where(last_lane, pltpu.roll(centre, 1, 0), centre)
        up_w = HALF * (centre + jnp.where(z_last, 0.0, pltpu.roll(above, 127, 1)))
        down_w = HALF * (centre + jnp.where(z_first, 0.0, pltpu.roll(below, 1, 1)))
        dg[x, r : r + 8, :] = up_w + down_w
        wzp[x, r : r + 8, :] = jnp.where(z_last, 0.0, up_w)
        wzm[x, r : r + 8, :] = jnp.where(z_first, 0.0, down_w)

    def add_diagonal(x, r):
        s = slice(r, r + 8)
        dg[x, s, :] = dg[x, s, :] + ((wx[x - 1, s, :] + wx[x, s, :]) + (wy[x, r - 4 : r + 4, :] + wy[x, s, :]))

    def apply(f, x, r):
        s = slice(r, r + 8)
        centre = f[x, s, :]
        out = dg[x, s, :] * centre
        out = out - wx[x - 1, s, :] * f[x - 1, s, :]
        out = out - wx[x, s, :] * f[x + 1, s, :]
        out = out - wy[x, r - 4 : r + 4, :] * f[x, r - 4 : r + 4, :]
        out = out - wy[x, s, :] * f[x, r + 4 : r + 12, :]
        out = out - wzm[x, s, :] * z_down(f, x, r, centre)
        out = out - wzp[x, s, :] * z_up(f, x, r, centre)
        return centre, out

    def chunks(first, last):
        return tuple(range(R0 + 4 * first, R0 + 4 * last, 8))

    def over(planes, body, carry, unroll=1):
        if not isinstance(planes, range):
            for x in planes:
                carry = body(x, carry)
            return carry
        first, steps = planes.start, len(planes) // unroll

        def several(i, carry):
            for u in range(unroll):
                carry = body(first + i * unroll + u, carry)
            return carry

        return lax.fori_loop(0, steps, several, carry)

    def step(f, w, counted):
        def run(planes, rows, acc, unroll=1):
            def body(x, acc):
                own = (zero,) * counted
                for r in rows:
                    centre, out = apply(f, x, r)
                    if f is up:
                        out = rb[x, r : r + 8, :] - SCALE * out
                    if w is not None:
                        w[x, r : r + 8, :] = out
                    if acc is not None and counted == 1:
                        own = (own[0] + out * out,)
                    elif acc is not None:
                        own = (own[0] + centre * out, own[1] + out * out)
                return None if acc is None else tuple(a + o for a, o in zip(acc, own))

            if acc is None:
                over(planes, lambda x, c: (body(x, None), c)[1], 0, unroll)
                return None
            return over(planes, body, acc, unroll)

        return run

    def when(flag, fn):
        pl.when(flag)(fn)

    def two_steps(name, first, second, acc1, acc2, wait_x, wait_y, between):
        with jax.named_scope(name + "_in1"):
            acc1 = first(range(X0 + 1, X1 - 1), chunks(2, 29), acc1, 2)
        with jax.named_scope(name + "_in2"):
            acc2 = second(range(X0 + 2, X1 - 2), chunks(4, 27), acc2, 2)
        between()
        with jax.named_scope(name + "_waitx"):
            wait_x()
        with jax.named_scope(name + "_ringx"):
            acc1 = first((X0, X1 - 1), chunks(2, 29), acc1)
            when(has_low_x, lambda: first((X0 - 1,), chunks(2, 29), None))
            when(has_high_x, lambda: first((X1,), chunks(2, 29), None))
            acc2 = second((X0, X0 + 1, X1 - 2, X1 - 1), chunks(4, 27), acc2)
        with jax.named_scope(name + "_waity"):
            wait_y()
        with jax.named_scope(name + "_ringy1"):
            acc1 = first(range(X0, X1), chunks(0, 1) + chunks(30, 31), acc1, 4)
            when(has_low_x, lambda: first((X0 - 1,), chunks(0, 1) + chunks(30, 31), None))
            when(has_high_x, lambda: first((X1,), chunks(0, 1) + chunks(30, 31), None))
            when(has_low_y, lambda: first(range(X0, X1), chunks(-2, -1), None, 8))
            when(has_high_y, lambda: first(range(X0, X1), chunks(32, 33), None, 8))
        with jax.named_scope(name + "_ringy2"):
            acc2 = second(range(X0, X1), chunks(0, 3) + chunks(28, 31), acc2, 4)
        return acc1, acc2

    own = chunks(0, 31)
    inner = chunks(2, 29)
    ends = chunks(0, 1) + chunks(30, 31)

    def own_weights(x, c, with_x=True, diagonal=True):
        for r in own:
            if with_x:
                weights_x(x, r)
            weights_z(x, r)
        for r in own[:-1]:
            weights_y(x, r)
        weights_y(x, R1 - 8, 4)
        if diagonal:
            for r in inner:
                add_diagonal(x, r)
        return c

    with jax.named_scope("weights"):
        own_weights(X0, 0, diagonal=False)
        over(range(X0 + 1, X1 - 1), own_weights, 0, 2)
        own_weights(X1 - 1, 0, with_x=False, diagonal=False)

    def halo_weights():
        with jax.named_scope("wait_k"):
            arrived(0, kp, 2, every_way)
        with jax.named_scope("halo_weights"):
            for i in (X0 - 2, X0 - 1, X1 - 1, X1):
                for r in own:
                    weights_x(i, r)
            for x in (X0 - 1, X1):
                for r in own:
                    weights_z(x, r)
                    weights_y(x, r)
                weights_y(x, R0 - 4, 4)
                for r in own:
                    add_diagonal(x, r)
            for r in (R0 - 8, R1):
                weights_x(X0 - 1, r)

            def body(x, c):
                weights_y(x, R0 - 8, 8)
                weights_y(x, R1 - 4, 8)
                for r in (R0 - 8, R1):
                    weights_x(x, r)
                    weights_z(x, r)
                for r in (R0 - 8, R1) + ends:
                    add_diagonal(x, r)
                return c

            over(range(X0, X1), body, 0, 4)
            for x in (X0, X1 - 1):
                for r in inner:
                    add_diagonal(x, r)

    def wait_fields_x():
        arrived(1, up, 2, along_x)
        arrived(2, rb, 1, along_x)

    def wait_fields_y():
        arrived(1, up, 2, along_y + corners)
        arrived(2, rb, 1, along_y)

    pair = (zero, zero)
    (m0,), (m1, m2) = two_steps(
        "p1", step(up, rp, 1), step(rp, v1, 2), (zero,), pair, wait_fields_x, wait_fields_y, halo_weights
    )
    exchange(3, v1, 2, every_way)
    (m3, m4), (m5, m6) = two_steps(
        "p2", step(v1, v2, 2), step(v2, None, 2), pair, pair,
        lambda: arrived(3, v1, 2, along_x), lambda: arrived(3, v1, 2, along_y + corners), lambda: None,
    )
    moments = [m0, m1, m2, m3, m4, m5, m6]

    with jax.named_scope("moments"):
        stacked = zero
        for k, m in enumerate(moments):
            stacked = jnp.where(sub == k, jnp.sum(m, axis=0, keepdims=True), stacked)
        high, low = split_sum(stacked, 1)
        mine = jnp.sum(jnp.where(lane == sub, high, jnp.where(lane == sub + 8, low, 0.0)), axis=0, keepdims=True)
    place = gx * ngy + gy
    row[...] = mine
    gath[pl.ds(place, 1), :] = mine
    pl.semaphore_wait(ready, ngx - 1)
    with jax.named_scope("gsend"):
        for dx, dy in far_first(ngx, ngy):
            pltpu.make_async_remote_copy(
                src_ref=row, dst_ref=gath.at[pl.ds(place, 1), :], send_sem=gsend, recv_sem=grecv,
                device_id=(lax.rem(gx + dx, ngx), lax.rem(gy + dy, ngy)), device_id_type=MESH,
            ).start()
    every = pltpu.make_async_remote_copy(
        src_ref=gath.at[0 : count - 1, :], dst_ref=gath.at[0 : count - 1, :], send_sem=gsend, recv_sem=grecv,
        device_id=(gx, gy), device_id_type=MESH,
    )
    with jax.named_scope("gwait"):
        every.wait_recv()
    with jax.named_scope("solve"):
        high, low = split_sum(gath[...], 0)
        lane1 = lax.broadcasted_iota(jnp.int32, (1, 128), 1)

        def pick(v, k):
            return jnp.sum(jnp.where(lane1 == k, v, 0.0), axis=1, keepdims=True)

        m = [renorm(pick(high, k), pick(low, k) + pick(high + low, k + 8)) for k in range(7)]
        (y1, y2, y3), rest = normal_equations(m)
        est_ref[...] = jnp.broadcast_to(jnp.sqrt(jnp.maximum(rest, 0.0)), (1, 128))
        y1, y2, y3 = (jnp.broadcast_to(y, (8, 128)) for y in (y1, y2, y3))

    def combine(x, c):
        for r in own:
            s = slice(r, r + 8)
            sol_ref[x - X0, r - R0 : r - R0 + 8, :] = up[x, s, :] + (
                y1 * rp[x, s, :] + (y2 * v1[x, s, :] + y3 * v2[x, s, :])
            )
        return c

    with jax.named_scope("final"):
        over(range(X0, X1), combine, 0, 2)
    every.wait_send()
    sent(0, kp, 2, every_way)
    sent(1, up, 2, every_way)
    sent(2, rb, 1, faces)
    sent(3, v1, 2, every_way)


def local(ngx, ngy, right_side, start_guess, conductivity):
    field = pltpu.VMEM((PLANES, ROWS, 128), F32)
    sem = pltpu.SemaphoreType
    sol, est = pl.pallas_call(
        functools.partial(kernel, ngx, ngy),
        out_shape=(jax.ShapeDtypeStruct((32, 128, 128), F32), jax.ShapeDtypeStruct((1, 128), F32)),
        in_specs=[pl.BlockSpec(memory_space=pltpu.HBM)] * 3,
        out_specs=(pl.BlockSpec(memory_space=pltpu.VMEM), pl.BlockSpec(memory_space=pltpu.VMEM)),
        scratch_shapes=[field] * 11 + [
            pltpu.VMEM((1, 128), F32),
            pltpu.VMEM((ngx * ngy, 128), F32),
            sem.DMA((3, 4)), sem.DMA((4, 8)), sem.DMA((4, 8)), sem.DMA, sem.DMA, sem.REGULAR,
        ],
        compiler_params=pltpu.CompilerParams(
            collective_id=0, has_side_effects=True, vmem_limit_bytes=50 * 2**20
        ),
    )(right_side, start_guess, conductivity)
    return sol.reshape(32, 32, 512), est[0, 0]


def solution(mesh):
    return jax.shard_map(
        functools.partial(local, mesh.shape["gx"], mesh.shape["gy"]),
        mesh=mesh,
        in_specs=(P("gx", "gy", None),) * 3,
        out_specs=(P("gx", "gy", None), P()),
        check_vma=False,
    )
```

time: 40.2 us -> 40.3 us (level)
  no operation moved by 1% of the time
where the time goes in v3:
time: 40.3 us; the launch traced here: 40.1 us
  Pallas kernels  36.8 us (91%)
  between operations  1.8 us (4%)
  local copies, waits for them, and re-layouts  1.49 us (4%)
    pallas_call x1, Pallas kernels, local(): pl.pallas_call(functools.partial(kernel, ngx, ngy), out_shape=(jax.ShapeD...  36.8 us
    reshape x1, local copies, waits for them, and re-layouts, local(): return (sol.reshape(32, 32, 512), est[0, 0])  1.49 us

profile of v3, /device:TPU:1, one launch (start us, length us, event | category | flops | bytes accessed | tf_op | source)
XLA Modules:
  0.0 40.1 jit_solution(11011982043823996488)
XLA Ops:
  0.6 36.8 %shard_map.50 = (f32[32,128,128]{2,1,0:T(8,128)S(1)}, f32[1,128]{1,0:T(1,128)S(1)}) custom-call(f32[32,32,512]{2,1,0:T(8,128)} %rhs_hbm.1, f32[32,32,512]{2,1,0:T(8,128)} %x0_hbm.1, f32[32,32,512]{2,1,0:T(8,128)} %k_hbm.1), custom_call_target="tpu_custom_call" | custom-call | tf_op jit(solution)/shard_map/pallas_call | solution.py:467
  37.5 1.5 %reshape.7 = f32[32,32,512]{2,1,0:T(8,128)} reshape(f32[32,128,128]{2,1,0:T(8,128)S(1)} %get-tuple-element.4) | data formatting | bytes 4194304 | tf_op jit(solution)/shard_map/reshape | solution.py:481

commit v4 on v3

--- a/solution.py
+++ b/solution.py
@@ -14,6 +14,7 @@
 X0, X1 = 2, 34
 R0, R1 = 16, 144
 PLANES, ROWS = 36, 160
+UW, U1, U2, UY = 5, 5, 4, 8
 
 
 def renorm(a, b):
@@ -215,12 +216,6 @@
     with jax.named_scope("barrier"):
         pl.semaphore_wait(barrier, len(greet))
         exchange(0, kp, 2, every_way)
-        for copy in loads[4:8]:
-            copy.wait()
-        exchange(1, up, 2, every_way)
-        for copy in loads[8:]:
-            copy.wait()
-        exchange(2, rb, 1, faces)
         for d in range(1, ngx):
             pl.semaphore_signal(ready, inc=1, device_id=(lax.rem(gx + d, ngx), gy), device_id_type=MESH)
 
@@ -294,47 +289,43 @@
                     centre, out = apply(f, x, r)
                     if f is up:
                         out = rb[x, r : r + 8, :] - SCALE * out
+                    inside = True
+                    for at, low, high, below, beyond in (
+                        (x, X0, X1, has_low_x, has_high_x), (r, R0, R1, has_low_y, has_high_y)
+                    ):
+                        if isinstance(at, int) and not low <= at < high:
+                            inside = False
+                            out = jnp.where(below if at < low else beyond, out, 0.0)
                     if w is not None:
                         w[x, r : r + 8, :] = out
-                    if acc is not None and counted == 1:
+                    if inside and counted == 1:
                         own = (own[0] + out * out,)
-                    elif acc is not None:
+                    elif inside:
                         own = (own[0] + centre * out, own[1] + out * out)
-                return None if acc is None else tuple(a + o for a, o in zip(acc, own))
-
-            if acc is None:
-                over(planes, lambda x, c: (body(x, None), c)[1], 0, unroll)
-                return None
+                return tuple(a + o for a, o in zip(acc, own))
+
             return over(planes, body, acc, unroll)
 
         return run
-
-    def when(flag, fn):
-        pl.when(flag)(fn)
 
     def two_steps(name, first, second, acc1, acc2, wait_x, wait_y, between):
         with jax.named_scope(name + "_in1"):
-            acc1 = first(range(X0 + 1, X1 - 1), chunks(2, 29), acc1, 2)
+            acc1 = first(range(X0 + 1, X1 - 1), chunks(2, 29), acc1, U1)
         with jax.named_scope(name + "_in2"):
-            acc2 = second(range(X0 + 2, X1 - 2), chunks(4, 27), acc2, 2)
+            acc2 = second(range(X0 + 2, X1 - 2), chunks(4, 27), acc2, U2)
         between()
         with jax.named_scope(name + "_waitx"):
             wait_x()
         with jax.named_scope(name + "_ringx"):
-            acc1 = first((X0, X1 - 1), chunks(2, 29), acc1)
-            when(has_low_x, lambda: first((X0 - 1,), chunks(2, 29), None))
-            when(has_high_x, lambda: first((X1,), chunks(2, 29), None))
+            acc1 = first((X0 - 1, X0, X1 - 1, X1), chunks(2, 29), acc1)
             acc2 = second((X0, X0 + 1, X1 - 2, X1 - 1), chunks(4, 27), acc2)
         with jax.named_scope(name + "_waity"):
             wait_y()
         with jax.named_scope(name + "_ringy1"):
-            acc1 = first(range(X0, X1), chunks(0, 1) + chunks(30, 31), acc1, 4)
-            when(has_low_x, lambda: first((X0 - 1,), chunks(0, 1) + chunks(30, 31), None))
-            when(has_high_x, lambda: first((X1,), chunks(0, 1) + chunks(30, 31), None))
-            when(has_low_y, lambda: first(range(X0, X1), chunks(-2, -1), None, 8))
-            when(has_high_y, lambda: first(range(X0, X1), chunks(32, 33), None, 8))
+            acc1 = first((X0 - 1, X1), chunks(0, 1) + chunks(30, 31), acc1)
+            acc1 = first(range(X0, X1), chunks(-2, 1) + chunks(30, 33), acc1, UY)
         with jax.named_scope(name + "_ringy2"):
-            acc2 = second(range(X0, X1), chunks(0, 3) + chunks(28, 31), acc2, 4)
+            acc2 = second(range(X0, X1), chunks(0, 3) + chunks(28, 31), acc2, UY)
         return acc1, acc2
 
     own = chunks(0, 31)
@@ -354,10 +345,18 @@
                 add_diagonal(x, r)
         return c
 
-    with jax.named_scope("weights"):
+    with jax.named_scope("weights1"):
         own_weights(X0, 0, diagonal=False)
-        over(range(X0 + 1, X1 - 1), own_weights, 0, 2)
+        over(range(X0 + 1, X0 + 11), own_weights, 0, UW)
+        for copy in loads[4:8]:
+            copy.wait()
+        exchange(1, up, 2, every_way)
+    with jax.named_scope("weights2"):
+        over(range(X0 + 11, X1 - 1), own_weights, 0, UW)
         own_weights(X1 - 1, 0, with_x=False, diagonal=False)
+        for copy in loads[8:]:
+            copy.wait()
+        exchange(2, rb, 1, faces)
 
     def halo_weights():
         with jax.named_scope("wait_k"):
@@ -386,7 +385,7 @@
                     add_diagonal(x, r)
                 return c
 
-            over(range(X0, X1), body, 0, 4)
+            over(range(X0, X1), body, 0, UY)
             for x in (X0, X1 - 1):
                 for r in inner:
                     add_diagonal(x, r)

time: 40.3 us -> 37.5 us (0.931)
  Pallas kernels: 36.8 us -> 34 us
    pallas_call x1, Pallas kernels: 36.8 us -> 34 us  [local(): pl.pallas_call(functools.partial(kernel, ngx, ngy), out_shape=(jax.ShapeD...]
where the time goes in v4:
time: 37.5 us; the launch traced here: 37.3 us
  Pallas kernels  34 us (91%)
  between operations  1.8 us (5%)
  local copies, waits for them, and re-layouts  1.49 us (4%)
    pallas_call x1, Pallas kernels, local(): pl.pallas_call(functools.partial(kernel, ngx, ngy), out_shape=(jax.ShapeD...  34 us
    reshape x1, local copies, waits for them, and re-layouts, local(): return (sol.reshape(32, 32, 512), est[0, 0])  1.49 us

profile of v4, /device:TPU:1, one launch (start us, length us, event | category | flops | bytes accessed | tf_op | source)
XLA Modules:
  0.0 37.3 jit_solution(8740445298902186701)
XLA Ops:
  0.6 34.0 %shard_map.50 = (f32[32,128,128]{2,1,0:T(8,128)S(1)}, f32[1,128]{1,0:T(1,128)S(1)}) custom-call(f32[32,32,512]{2,1,0:T(8,128)} %rhs_hbm.1, f32[32,32,512]{2,1,0:T(8,128)} %x0_hbm.1, f32[32,32,512]{2,1,0:T(8,128)} %k_hbm.1), custom_call_target="tpu_custom_call" | custom-call | tf_op jit(solution)/shard_map/pallas_call | solution.py:466
  34.7 1.5 %reshape.7 = f32[32,32,512]{2,1,0:T(8,128)} reshape(f32[32,128,128]{2,1,0:T(8,128)S(1)} %get-tuple-element.4) | data formatting | bytes 4194304 | tf_op jit(solution)/shard_map/reshape | solution.py:480

commit v5 on v4

--- a/solution.py
+++ b/solution.py
@@ -11,10 +11,10 @@
 F32 = jnp.float32
 SCALE = 64.0
 HALF = 0.5 / SCALE
-X0, X1 = 2, 34
+X0, X1 = 3, 35
 R0, R1 = 16, 144
-PLANES, ROWS = 36, 160
-UW, U1, U2, UY = 5, 5, 4, 8
+PLANES, ROWS = 38, 160
+UW, U1, U2, U3, UY = 5, 5, 4, 4, 8
 
 
 def renorm(a, b):
@@ -104,18 +104,17 @@
     return sorted(offsets, key=lambda o: -(ring(o[0] // 2) + ring(o[1] // 4) + ring(o[1] % 4)))
 
 
-def extent(step, low, high, depth, outside):
+def extent(step, low, high, near, far, outside):
     if step == 0:
         return slice(low, high)
     if outside:
-        return slice(low - depth, low) if step > 0 else slice(high, high + depth)
-    return slice(high - depth, high) if step > 0 else slice(low, low + depth)
-
-
-def piece(ref, sx, sy, depth, outside):
-    if sx and sy:
-        depth = 1
-    return ref.at[extent(sx, X0, X1, depth, outside), extent(sy, R0, R1, 4 * depth, outside), :]
+        return slice(low - far, low - near) if step > 0 else slice(high + near, high + far)
+    return slice(high - far, high - near) if step > 0 else slice(low + near, low + far)
+
+
+def piece(ref, sx, sy, layers, outside):
+    near, far = (0, 2) if sx and sy else layers
+    return ref.at[extent(sx, X0, X1, near, far, outside), extent(sy, R0, R1, 4 * near, 4 * far, outside), :]
 
 
 def kernel(
@@ -159,55 +158,56 @@
         def _():
             def fill(i, c):
                 for f in fields:
-                    for x in (at, at + 1):
-                        f[x, pl.ds(pl.multiple_of(8 + 8 * i, 8), 8), :] = zero
+                    for x in range(at, at + 3):
+                        f[x, pl.ds(pl.multiple_of(8 * i, 8), 8), :] = zero
                 return c
 
-            lax.fori_loop(0, 18, fill, 0)
-
-    for at, inside in ((R0 - 8, has_low_y), (R1, has_high_y)):
+            lax.fori_loop(0, ROWS // 8, fill, 0)
+
+    for at, inside in ((0, has_low_y), (R1, has_high_y)):
 
         @pl.when(jnp.logical_not(inside))
         def _():
             def fill(x, c):
                 for f in fields:
-                    f[x, at : at + 8, :] = zero
+                    for r in (at, at + 8):
+                        f[x, r : r + 8, :] = zero
                 return c
 
             lax.fori_loop(0, PLANES, fill, 0)
 
-    def copy_of(e, f, depth, i):
+    def copy_of(e, f, layers, i):
         sx, sy = dirs[i][:2]
         return pltpu.make_async_remote_copy(
-            src_ref=piece(f, sx, sy, depth, False), dst_ref=piece(f, sx, sy, depth, True),
+            src_ref=piece(f, sx, sy, layers, False), dst_ref=piece(f, sx, sy, layers, True),
             send_sem=send_sem.at[e, i], recv_sem=recv_sem.at[e, i],
             device_id={"gx": lax.rem(gx + sx + ngx, ngx), "gy": lax.rem(gy + sy + ngy, ngy)},
             device_id_type=MESH,
         )
 
-    def exchange(e, f, depth, which):
+    def exchange(e, f, layers, which):
         for i in which:
 
             @pl.when(dirs[i][2])
             def _():
-                copy_of(e, f, depth, i).start()
-
-    def arrived(e, f, depth, which):
+                copy_of(e, f, layers, i).start()
+
+    def arrived(e, f, layers, which):
         for i in which:
 
             @pl.when(dirs[i][3])
             def _():
-                copy_of(e, f, depth, i).wait_recv()
-
-    def sent(e, f, depth, which):
+                copy_of(e, f, layers, i).wait_recv()
+
+    def sent(e, f, layers, which):
         for i in which:
 
             @pl.when(dirs[i][2])
             def _():
-                copy_of(e, f, depth, i).wait_send()
+                copy_of(e, f, layers, i).wait_send()
 
     along_y, along_x, corners = (0, 1), (2, 3), (4, 5, 6, 7)
-    every_way = along_y + along_x + corners
+    every_way = corners + along_y + along_x
     faces = along_y + along_x
 
     with jax.named_scope("load_k"):
@@ -215,7 +215,7 @@
             copy.wait()
     with jax.named_scope("barrier"):
         pl.semaphore_wait(barrier, len(greet))
-        exchange(0, kp, 2, every_way)
+        exchange(0, kp, (0, 1), faces)
         for d in range(1, ngx):
             pl.semaphore_signal(ready, inc=1, device_id=(lax.rem(gx + d, ngx), gy), device_id_type=MESH)
 
@@ -264,8 +264,8 @@
         out = out - wzp[x, s, :] * z_up(f, x, r, centre)
         return centre, out
 
-    def chunks(first, last):
-        return tuple(range(R0 + 4 * first, R0 + 4 * last, 8))
+    def chunks(first, last, counts=None):
+        return tuple((r, 3 if counts is None else counts) for r in range(R0 + 4 * first, R0 + 4 * last, 8))
 
     def over(planes, body, carry, unroll=1):
         if not isinstance(planes, range):
@@ -285,7 +285,7 @@
         def run(planes, rows, acc, unroll=1):
             def body(x, acc):
                 own = (zero,) * counted
-                for r in rows:
+                for r, layers in rows:
                     centre, out = apply(f, x, r)
                     if f is up:
                         out = rb[x, r : r + 8, :] - SCALE * out
@@ -298,39 +298,22 @@
                             out = jnp.where(below if at < low else beyond, out, 0.0)
                     if w is not None:
                         w[x, r : r + 8, :] = out
-                    if inside and counted == 1:
-                        own = (own[0] + out * out,)
-                    elif inside:
-                        own = (own[0] + centre * out, own[1] + out * out)
+                    if not inside or layers == 0:
+                        continue
+                    terms = (out * out,) if counted == 1 else (centre * out, out * out)
+                    if layers < 3:
+                        terms = tuple(jnp.where((sub < 4) == (layers == 1), t, 0.0) for t in terms)
+                    own = tuple(o + t for o, t in zip(own, terms))
                 return tuple(a + o for a, o in zip(acc, own))
 
             return over(planes, body, acc, unroll)
 
         return run
 
-    def two_steps(name, first, second, acc1, acc2, wait_x, wait_y, between):
-        with jax.named_scope(name + "_in1"):
-            acc1 = first(range(X0 + 1, X1 - 1), chunks(2, 29), acc1, U1)
-        with jax.named_scope(name + "_in2"):
-            acc2 = second(range(X0 + 2, X1 - 2), chunks(4, 27), acc2, U2)
-        between()
-        with jax.named_scope(name + "_waitx"):
-            wait_x()
-        with jax.named_scope(name + "_ringx"):
-            acc1 = first((X0 - 1, X0, X1 - 1, X1), chunks(2, 29), acc1)
-            acc2 = second((X0, X0 + 1, X1 - 2, X1 - 1), chunks(4, 27), acc2)
-        with jax.named_scope(name + "_waity"):
-            wait_y()
-        with jax.named_scope(name + "_ringy1"):
-            acc1 = first((X0 - 1, X1), chunks(0, 1) + chunks(30, 31), acc1)
-            acc1 = first(range(X0, X1), chunks(-2, 1) + chunks(30, 33), acc1, UY)
-        with jax.named_scope(name + "_ringy2"):
-            acc2 = second(range(X0, X1), chunks(0, 3) + chunks(28, 31), acc2, UY)
-        return acc1, acc2
-
-    own = chunks(0, 31)
-    inner = chunks(2, 29)
-    ends = chunks(0, 1) + chunks(30, 31)
+    own = [r for r, _ in chunks(0, 31)]
+    inner = [r for r, _ in chunks(2, 29)]
+    ends = (R0, R1 - 8)
+    outer = (R0 - 8, R1)
 
     def own_weights(x, c, with_x=True, diagonal=True):
         for r in own:
@@ -350,63 +333,105 @@
         over(range(X0 + 1, X0 + 11), own_weights, 0, UW)
         for copy in loads[4:8]:
             copy.wait()
-        exchange(1, up, 2, every_way)
+        exchange(1, up, (0, 1), faces)
+        exchange(2, kp, (1, 3), every_way)
     with jax.named_scope("weights2"):
         over(range(X0 + 11, X1 - 1), own_weights, 0, UW)
         own_weights(X1 - 1, 0, with_x=False, diagonal=False)
         for copy in loads[8:]:
             copy.wait()
-        exchange(2, rb, 1, faces)
-
-    def halo_weights():
-        with jax.named_scope("wait_k"):
-            arrived(0, kp, 2, every_way)
-        with jax.named_scope("halo_weights"):
-            for i in (X0 - 2, X0 - 1, X1 - 1, X1):
-                for r in own:
-                    weights_x(i, r)
-            for x in (X0 - 1, X1):
-                for r in own:
-                    weights_z(x, r)
-                    weights_y(x, r)
-                weights_y(x, R0 - 4, 4)
-                for r in own:
-                    add_diagonal(x, r)
-            for r in (R0 - 8, R1):
-                weights_x(X0 - 1, r)
-
-            def body(x, c):
-                weights_y(x, R0 - 8, 8)
-                weights_y(x, R1 - 4, 8)
-                for r in (R0 - 8, R1):
-                    weights_x(x, r)
-                    weights_z(x, r)
-                for r in (R0 - 8, R1) + ends:
-                    add_diagonal(x, r)
-                return c
-
-            over(range(X0, X1), body, 0, UY)
-            for x in (X0, X1 - 1):
-                for r in inner:
-                    add_diagonal(x, r)
-
-    def wait_fields_x():
-        arrived(1, up, 2, along_x)
-        arrived(2, rb, 1, along_x)
-
-    def wait_fields_y():
-        arrived(1, up, 2, along_y + corners)
-        arrived(2, rb, 1, along_y)
-
-    pair = (zero, zero)
-    (m0,), (m1, m2) = two_steps(
-        "p1", step(up, rp, 1), step(rp, v1, 2), (zero,), pair, wait_fields_x, wait_fields_y, halo_weights
-    )
-    exchange(3, v1, 2, every_way)
-    (m3, m4), (m5, m6) = two_steps(
-        "p2", step(v1, v2, 2), step(v2, None, 2), pair, pair,
-        lambda: arrived(3, v1, 2, along_x), lambda: arrived(3, v1, 2, along_y + corners), lambda: None,
-    )
+
+    residual = step(up, rp, 1)
+    m0 = (zero,)
+    with jax.named_scope("p1_in"):
+        m0 = residual(range(X0 + 1, X1 - 1), chunks(2, 29), m0, U1)
+    with jax.named_scope("wait_k"):
+        arrived(0, kp, (0, 1), faces)
+    with jax.named_scope("edge_weights"):
+        for r in own:
+            weights_x(X0 - 1, r)
+            weights_x(X1 - 1, r)
+
+        def edge(x, c):
+            weights_y(x, R0 - 4, 4)
+            weights_y(x, R1 - 4, 4)
+            for r in ends:
+                add_diagonal(x, r)
+            return c
+
+        over(range(X0, X1), edge, 0, UY)
+        for x in (X0, X1 - 1):
+            for r in inner:
+                add_diagonal(x, r)
+    with jax.named_scope("p1_waitx"):
+        arrived(1, up, (0, 1), along_x)
+    with jax.named_scope("p1_ringx"):
+        m0 = residual((X0, X1 - 1), chunks(2, 29), m0)
+    with jax.named_scope("p1_waity"):
+        arrived(1, up, (0, 1), along_y)
+    with jax.named_scope("p1_ringy"):
+        m0 = residual(range(X0, X1), chunks(0, 1) + chunks(30, 31), m0, UY)
+        exchange(3, rp, (0, 3), every_way)
+
+    powers = (step(rp, v1, 2), step(v1, v2, 2), step(v2, None, 2))
+    rows = (chunks(1, 30), chunks(2, 29), chunks(3, 28))
+    acc = [(zero, zero)] * 3
+    depth = (1, 2, 4)
+    for n in range(3):
+        with jax.named_scope("p2_in%d" % n):
+            acc[n] = powers[n](range(X0 + depth[n], X1 - depth[n]), rows[n], acc[n], (U1, U2, U3)[n])
+    with jax.named_scope("wait_k2"):
+        arrived(2, kp, (1, 3), every_way)
+    with jax.named_scope("halo_weights"):
+        beside = (X0 - 2, X0 - 1, X1, X1 + 1)
+        for i in (X0 - 3, X0 - 2, X1, X1 + 1):
+            for r in own:
+                weights_x(i, r)
+        for x in beside:
+            for r in own:
+                weights_z(x, r)
+                weights_y(x, r)
+            weights_y(x, R0 - 4, 4)
+            for r in own:
+                add_diagonal(x, r)
+
+        def halo(x, c, with_x=True):
+            weights_y(x, R0 - 12, 8)
+            weights_y(x, R1, 8)
+            for r in outer:
+                weights_x(x, r)
+                weights_z(x, r)
+                add_diagonal(x, r)
+            return c
+
+        for r in outer:
+            weights_x(X0 - 2, r)
+        halo(X0 - 1, 0)
+        over(range(X0, X1), halo, 0, UY)
+        halo(X1, 0)
+    with jax.named_scope("p2_waitx"):
+        arrived(3, rp, (0, 3), along_x)
+    with jax.named_scope("p2_ringx"):
+        for n in range(3):
+            low, high = X0 - 2 + n, X1 + 2 - n
+            acc[n] = powers[n](tuple(range(low, X0 + depth[n])) + tuple(range(X1 - depth[n], high)), rows[n], acc[n])
+    with jax.named_scope("p2_waity"):
+        arrived(3, rp, (0, 3), along_y + corners)
+    halos = chunks(-2, -1, 0) + chunks(32, 33, 0)
+    with jax.named_scope("p2_ringy0"):
+        lines = chunks(0, 1, 1) + chunks(30, 31, 2)
+        acc[0] = powers[0](beside, lines, acc[0])
+        acc[0] = powers[0]((X0 - 1, X1), halos, acc[0])
+        acc[0] = powers[0](range(X0, X1), lines + halos, acc[0], UY)
+    with jax.named_scope("p2_ringy1"):
+        lines = chunks(0, 1) + chunks(30, 31)
+        acc[1] = powers[1]((X0 - 1, X1), lines, acc[1])
+        acc[1] = powers[1](range(X0, X1), lines + halos, acc[1], UY)
+    with jax.named_scope("p2_ringy2"):
+        lines = chunks(0, 1) + chunks(2, 3, 1) + chunks(28, 29, 2) + chunks(30, 31)
+        acc[2] = powers[2](range(X0, X1), lines, acc[2], UY)
+    (m1, m2), (m3, m4), (m5, m6) = acc
+    m0 = m0[0]
     moments = [m0, m1, m2, m3, m4, m5, m6]
 
     with jax.named_scope("moments"):
@@ -454,10 +479,10 @@
     with jax.named_scope("final"):
         over(range(X0, X1), combine, 0, 2)
     every.wait_send()
-    sent(0, kp, 2, every_way)
-    sent(1, up, 2, every_way)
-    sent(2, rb, 1, faces)
-    sent(3, v1, 2, every_way)
+    sent(0, kp, (0, 1), faces)
+    sent(1, up, (0, 1), faces)
+    sent(2, kp, (1, 3), every_way)
+    sent(3, rp, (0, 3), every_way)
 
 
 def local(ngx, ngy, right_side, start_guess, conductivity):

time: 37.5 us -> 35.5 us (0.947)
  Pallas kernels: 34 us -> 32.1 us
    pallas_call x1, Pallas kernels: 34 us -> 32.1 us  [local(): pl.pallas_call(functools.partial(kernel, ngx, ngy), out_shape=(jax.ShapeD...]
where the time goes in v5:
time: 35.5 us; the launch traced here: 35.4 us
  Pallas kernels  32.1 us (90%)
  between operations  1.8 us (5%)
  local copies, waits for them, and re-layouts  1.49 us (4%)
    pallas_call x1, Pallas kernels, local(): pl.pallas_call(functools.partial(kernel, ngx, ngy), out_shape=(jax.ShapeD...  32.1 us
    reshape x1, local copies, waits for them, and re-layouts, local(): return (sol.reshape(32, 32, 512), est[0, 0])  1.49 us

profile of v5, /device:TPU:1, one launch (start us, length us, event | category | flops | bytes accessed | tf_op | source)
XLA Modules:
  0.0 35.4 jit_solution(12847999704954975517)
XLA Ops:
  0.6 32.1 %shard_map.50 = (f32[32,128,128]{2,1,0:T(8,128)S(1)}, f32[1,128]{1,0:T(1,128)S(1)}) custom-call(f32[32,32,512]{2,1,0:T(8,128)} %rhs_hbm.1, f32[32,32,512]{2,1,0:T(8,128)} %x0_hbm.1, f32[32,32,512]{2,1,0:T(8,128)} %k_hbm.1), custom_call_target="tpu_custom_call" | custom-call | tf_op jit(solution)/shard_map/pallas_call | solution.py:491
  32.7 1.5 %reshape.7 = f32[32,32,512]{2,1,0:T(8,128)} reshape(f32[32,128,128]{2,1,0:T(8,128)S(1)} %get-tuple-element.4) | data formatting | bytes 4194304 | tf_op jit(solution)/shard_map/reshape | solution.py:505

commit v6 on v5

--- a/solution.py
+++ b/solution.py
@@ -124,6 +124,14 @@
     load_sem, send_sem, recv_sem, gsend, grecv, ready,
 ):
     gx, gy = lax.axis_index("gx"), lax.axis_index("gy")
+    xs, ys = [lax.rem(gx + d, ngx) for d in range(ngx)], [lax.rem(gy + d, ngy) for d in range(ngy)]
+    barrier = pltpu.get_barrier_semaphore()
+    near = [(0, 1), (0, ngy - 1), (1, 0), (ngx - 1, 0), (1, 1), (1, ngy - 1), (ngx - 1, 1), (ngx - 1, ngy - 1)]
+    greet = near + [(d, 0) for d in range(2, ngx - 1)] + [(0, d) for d in range(2, ngy - 1)]
+    for dx, dy in greet:
+        pl.semaphore_signal(
+            barrier, inc=1, device_id=(xs[dx], ys[dy]), device_id_type=MESH
+        )
     count = ngx * ngy
     loads = []
     for i, (src, dst) in enumerate(((k_hbm, kp), (x0_hbm, up), (rhs_hbm, rb))):
@@ -136,17 +144,8 @@
                     load_sem.at[i, q],
                 )
             )
-    for copy in loads:
+    for copy in loads[:8]:
         copy.start()
-
-    barrier = pltpu.get_barrier_semaphore()
-    greet = [(d, 0) for d in range(1, ngx)] + [(0, d) for d in range(1, ngy)]
-    greet += [(1, 1), (1, ngy - 1), (ngx - 1, 1), (ngx - 1, ngy - 1)]
-    for dx, dy in greet:
-        pl.semaphore_signal(
-            barrier, inc=1, device_id=(lax.rem(gx + dx, ngx), lax.rem(gy + dy, ngy)), device_id_type=MESH
-        )
-
     dirs = directions(gx, gy, ngx, ngy)
     has_low_x, has_high_x, has_low_y, has_high_y = gx > 0, gx < ngx - 1, gy > 0, gy < ngy - 1
     fields = (kp, up, rp, v1, v2)
@@ -213,6 +212,8 @@
     with jax.named_scope("load_k"):
         for copy in loads[:4]:
             copy.wait()
+        for copy in loads[8:]:
+            copy.start()
     with jax.named_scope("barrier"):
         pl.semaphore_wait(barrier, len(greet))
         exchange(0, kp, (0, 1), faces)
@@ -367,11 +368,23 @@
         arrived(1, up, (0, 1), along_x)
     with jax.named_scope("p1_ringx"):
         m0 = residual((X0, X1 - 1), chunks(2, 29), m0)
-    with jax.named_scope("p1_waity"):
-        arrived(1, up, (0, 1), along_y)
-    with jax.named_scope("p1_ringy"):
-        m0 = residual(range(X0, X1), chunks(0, 1) + chunks(30, 31), m0, UY)
-        exchange(3, rp, (0, 3), every_way)
+    high_last = lax.rem(gy, 4) == 3
+    sides = (((0,), (5, 7), chunks(0, 1)), ((1,), (4, 6), chunks(30, 31)))
+
+    def residual_strips(order):
+        def run(m0):
+            for side in order:
+                with jax.named_scope("p1_waity%d" % side):
+                    arrived(1, up, (0, 1), sides[side][0])
+                with jax.named_scope("p1_ringy%d" % side):
+                    m0 = residual(tuple(range(X0, X1)), sides[side][2], m0)
+                    exchange(3, rp, (0, 3), sides[side][1] + (1 - side,))
+            return m0
+
+        return run
+
+    m0 = lax.cond(high_last, residual_strips((0, 1)), residual_strips((1, 0)), m0)
+    exchange(3, rp, (0, 3), along_x)
 
     powers = (step(rp, v1, 2), step(v1, v2, 2), step(v2, None, 2))
     rows = (chunks(1, 30), chunks(2, 29), chunks(3, 28))
@@ -415,21 +428,30 @@
         for n in range(3):
             low, high = X0 - 2 + n, X1 + 2 - n
             acc[n] = powers[n](tuple(range(low, X0 + depth[n])) + tuple(range(X1 - depth[n], high)), rows[n], acc[n])
-    with jax.named_scope("p2_waity"):
-        arrived(3, rp, (0, 3), along_y + corners)
-    halos = chunks(-2, -1, 0) + chunks(32, 33, 0)
-    with jax.named_scope("p2_ringy0"):
-        lines = chunks(0, 1, 1) + chunks(30, 31, 2)
-        acc[0] = powers[0](beside, lines, acc[0])
-        acc[0] = powers[0]((X0 - 1, X1), halos, acc[0])
-        acc[0] = powers[0](range(X0, X1), lines + halos, acc[0], UY)
-    with jax.named_scope("p2_ringy1"):
-        lines = chunks(0, 1) + chunks(30, 31)
-        acc[1] = powers[1]((X0 - 1, X1), lines, acc[1])
-        acc[1] = powers[1](range(X0, X1), lines + halos, acc[1], UY)
-    with jax.named_scope("p2_ringy2"):
-        lines = chunks(0, 1) + chunks(2, 3, 1) + chunks(28, 29, 2) + chunks(30, 31)
-        acc[2] = powers[2](range(X0, X1), lines, acc[2], UY)
+    strips = (
+        ((0, 4, 6), chunks(0, 1, 1), chunks(-2, -1, 0), chunks(0, 1), chunks(0, 1) + chunks(2, 3, 1)),
+        ((1, 5, 7), chunks(30, 31, 2), chunks(32, 33, 0), chunks(30, 31), chunks(28, 29, 2) + chunks(30, 31)),
+    )
+
+    def power_strips(order):
+        def run(acc):
+            acc = list(acc)
+            for side in order:
+                ways, line, halos, line1, line2 = strips[side]
+                with jax.named_scope("p2_waity%d" % side):
+                    arrived(3, rp, (0, 3), ways)
+                with jax.named_scope("p2_ringy%d" % side):
+                    acc[0] = powers[0](beside, line, acc[0])
+                    acc[0] = powers[0]((X0 - 1, X1), halos, acc[0])
+                    acc[0] = powers[0](tuple(range(X0, X1)), line + halos, acc[0])
+                    acc[1] = powers[1]((X0 - 1, X1), line1, acc[1])
+                    acc[1] = powers[1](tuple(range(X0, X1)), line1 + halos, acc[1])
+                    acc[2] = powers[2](tuple(range(X0, X1)), line2, acc[2])
+            return tuple(acc)
+
+        return run
+
+    acc = lax.cond(high_last, power_strips((0, 1)), power_strips((1, 0)), tuple(acc))
     (m1, m2), (m3, m4), (m5, m6) = acc
     m0 = m0[0]
     moments = [m0, m1, m2, m3, m4, m5, m6]
@@ -448,7 +470,7 @@
         for dx, dy in far_first(ngx, ngy):
             pltpu.make_async_remote_copy(
                 src_ref=row, dst_ref=gath.at[pl.ds(place, 1), :], send_sem=gsend, recv_sem=grecv,
-                device_id=(lax.rem(gx + dx, ngx), lax.rem(gy + dy, ngy)), device_id_type=MESH,
+                device_id=(xs[dx], ys[dy]), device_id_type=MESH,
             ).start()
     every = pltpu.make_async_remote_copy(
         src_ref=gath.at[0 : count - 1, :], dst_ref=gath.at[0 : count - 1, :], send_sem=gsend, recv_sem=grecv,
@@ -469,11 +491,12 @@
         y1, y2, y3 = (jnp.broadcast_to(y, (8, 128)) for y in (y1, y2, y3))
 
     def combine(x, c):
-        for r in own:
-            s = slice(r, r + 8)
-            sol_ref[x - X0, r - R0 : r - R0 + 8, :] = up[x, s, :] + (
-                y1 * rp[x, s, :] + (y2 * v1[x, s, :] + y3 * v2[x, s, :])
-            )
+        for y in range(0, 32, 8):
+            for q in range(4):
+                s = pl.ds(R0 + 4 * y + q, 8, stride=4)
+                sol_ref[x - X0, y : y + 8, q * 128 : (q + 1) * 128] = up[x, s, :] + (
+                    y1 * rp[x, s, :] + (y2 * v1[x, s, :] + y3 * v2[x, s, :])
+                )
         return c
 
     with jax.named_scope("final"):
@@ -490,7 +513,7 @@
     sem = pltpu.SemaphoreType
     sol, est = pl.pallas_call(
         functools.partial(kernel, ngx, ngy),
-        out_shape=(jax.ShapeDtypeStruct((32, 128, 128), F32), jax.ShapeDtypeStruct((1, 128), F32)),
+        out_shape=(jax.ShapeDtypeStruct((32, 32, 512), F32), jax.ShapeDtypeStruct((1, 128), F32)),
         in_specs=[pl.BlockSpec(memory_space=pltpu.HBM)] * 3,
         out_specs=(pl.BlockSpec(memory_space=pltpu.VMEM), pl.BlockSpec(memory_space=pltpu.VMEM)),
         scratch_shapes=[field] * 11 + [
@@ -502,7 +525,7 @@
             collective_id=0, has_side_effects=True, vmem_limit_bytes=50 * 2**20
         ),
     )(right_side, start_guess, conductivity)
-    return sol.reshape(32, 32, 512), est[0, 0]
+    return sol, est[0, 0]
 
 
 def solution(mesh):

time: 35.5 us -> 34 us (0.958)
  Pallas kernels: 32.1 us -> 30.8 us
    reshape x1 -> x0, local copies, waits for them, and re-layouts: 1.49 us -> none  [local(): return (sol.reshape(32, 32, 512), est[0, 0])]
    unnamed x0 -> x1, local copies, waits for them, and re-layouts: none -> 1.32 us
    pallas_call x1, Pallas kernels: 32.1 us -> 30.8 us  [local(): pl.pallas_call(functools.partial(kernel, ngx, ngy), out_shape=(jax.ShapeD...]
where the time goes in v6:
time: 34 us; the launch traced here: 33.9 us
  Pallas kernels  30.8 us (91%)
  between operations  1.8 us (5%)
  local copies, waits for them, and re-layouts  1.32 us (4%)
    pallas_call x1, Pallas kernels, local(): pl.pallas_call(functools.partial(kernel, ngx, ngy), out_shape=(jax.ShapeD...  30.8 us
    unnamed x1, local copies, waits for them, and re-layouts  1.32 us

profile of v6, /device:TPU:1, one launch (start us, length us, event | category | flops | bytes accessed | tf_op | source)
XLA Modules:
  0.0 33.9 jit_solution(10437018711205687511)
XLA Ops:
  0.6 30.8 %shard_map.50 = (f32[32,32,512]{2,1,0:T(8,128)S(1)}, f32[1,128]{1,0:T(1,128)S(1)}) custom-call(f32[32,32,512]{2,1,0:T(8,128)} %rhs_hbm.1, f32[32,32,512]{2,1,0:T(8,128)} %x0_hbm.1, f32[32,32,512]{2,1,0:T(8,128)} %k_hbm.1), custom_call_target="tpu_custom_call" | custom-call | tf_op jit(solution)/shard_map/pallas_call | solution.py:514
  31.4 1.3 %copy.7 = f32[32,32,512]{2,1,0:T(8,128)} copy(f32[32,32,512]{2,1,0:T(8,128)S(1)} %get-tuple-element.8) | data formatting | bytes 4194304

commit v7 on v6

--- a/solution.py
+++ b/solution.py
@@ -120,8 +120,8 @@
 def kernel(
     ngx, ngy,
     rhs_hbm, x0_hbm, k_hbm, sol_ref, est_ref,
-    kp, up, rb, rp, v1, v2, wx, wy, wzm, wzp, dg, row, gath,
-    load_sem, send_sem, recv_sem, gsend, grecv, ready,
+    kp, up, rb, rp, v1, v2, wx, wy, wzm, wzp, dg, row, gath, staged,
+    face_sem, load_sem, send_sem, recv_sem, gsend, grecv, ready,
 ):
     gx, gy = lax.axis_index("gx"), lax.axis_index("gy")
     xs, ys = [lax.rem(gx + d, ngx) for d in range(ngx)], [lax.rem(gy + d, ngy) for d in range(ngy)]
@@ -144,7 +144,19 @@
                     load_sem.at[i, q],
                 )
             )
-    for copy in loads[:8]:
+    face_loads = [
+        [
+            pltpu.make_async_copy(
+                src.at[:, layer : layer + 1, q * 128 : (q + 1) * 128],
+                staged.at[i, side, :, q : q + 1, :],
+                face_sem.at[i, side, q],
+            )
+            for side, layer in enumerate((0, 31))
+            for q in range(4)
+        ]
+        for i, src in enumerate((k_hbm, x0_hbm))
+    ]
+    for copy in face_loads[0] + face_loads[1] + loads[:8]:
         copy.start()
     dirs = directions(gx, gy, ngx, ngy)
     has_low_x, has_high_x, has_low_y, has_high_y = gx > 0, gx < ngx - 1, gy > 0, gy < ngy - 1
@@ -178,7 +190,8 @@
     def copy_of(e, f, layers, i):
         sx, sy = dirs[i][:2]
         return pltpu.make_async_remote_copy(
-            src_ref=piece(f, sx, sy, layers, False), dst_ref=piece(f, sx, sy, layers, True),
+            src_ref=staged.at[e, (sy + 1) // 2] if e < 2 and sx == 0 else piece(f, sx, sy, layers, False),
+            dst_ref=piece(f, sx, sy, layers, True),
             send_sem=send_sem.at[e, i], recv_sem=recv_sem.at[e, i],
             device_id={"gx": lax.rem(gx + sx + ngx, ngx), "gy": lax.rem(gy + sy + ngy, ngy)},
             device_id_type=MESH,
@@ -209,16 +222,23 @@
     every_way = corners + along_y + along_x
     faces = along_y + along_x
 
+    with jax.named_scope("load_face"):
+        for copy in face_loads[0]:
+            copy.wait()
+    with jax.named_scope("barrier"):
+        pl.semaphore_wait(barrier, len(greet))
+        exchange(0, kp, (0, 1), along_y)
+        for copy in face_loads[1]:
+            copy.wait()
+        exchange(1, up, (0, 1), along_y)
     with jax.named_scope("load_k"):
         for copy in loads[:4]:
             copy.wait()
+        exchange(0, kp, (0, 1), along_x)
         for copy in loads[8:]:
             copy.start()
-    with jax.named_scope("barrier"):
-        pl.semaphore_wait(barrier, len(greet))
-        exchange(0, kp, (0, 1), faces)
         for d in range(1, ngx):
-            pl.semaphore_signal(ready, inc=1, device_id=(lax.rem(gx + d, ngx), gy), device_id_type=MESH)
+            pl.semaphore_signal(ready, inc=1, device_id=(xs[d], gy), device_id_type=MESH)
 
     lane = lax.broadcasted_iota(jnp.int32, (8, 128), 1)
     sub = lax.broadcasted_iota(jnp.int32, (8, 128), 0)
@@ -268,24 +288,23 @@
     def chunks(first, last, counts=None):
         return tuple((r, 3 if counts is None else counts) for r in range(R0 + 4 * first, R0 + 4 * last, 8))
 
-    def over(planes, body, carry, unroll=1):
+    def over(planes, body, carry, unroll=1, start=None):
+        def several(planes, carry):
+            part = carry if start is None else start
+            for x in planes:
+                part = body(x, part)
+            return part if start is None else tuple(c + p for c, p in zip(carry, part))
+
         if not isinstance(planes, range):
-            for x in planes:
-                carry = body(x, carry)
-            return carry
+            return several(planes, carry)
         first, steps = planes.start, len(planes) // unroll
-
-        def several(i, carry):
-            for u in range(unroll):
-                carry = body(first + i * unroll + u, carry)
-            return carry
-
-        return lax.fori_loop(0, steps, several, carry)
+        return lax.fori_loop(
+            0, steps, lambda i, carry: several([first + i * unroll + u for u in range(unroll)], carry), carry
+        )
 
     def step(f, w, counted):
         def run(planes, rows, acc, unroll=1):
-            def body(x, acc):
-                own = (zero,) * counted
+            def body(x, own):
                 for r, layers in rows:
                     centre, out = apply(f, x, r)
                     if f is up:
@@ -305,9 +324,9 @@
                     if layers < 3:
                         terms = tuple(jnp.where((sub < 4) == (layers == 1), t, 0.0) for t in terms)
                     own = tuple(o + t for o, t in zip(own, terms))
-                return tuple(a + o for a, o in zip(acc, own))
-
-            return over(planes, body, acc, unroll)
+                return own
+
+            return over(planes, body, acc, unroll, (zero,) * counted)
 
         return run
 
@@ -334,7 +353,7 @@
         over(range(X0 + 1, X0 + 11), own_weights, 0, UW)
         for copy in loads[4:8]:
             copy.wait()
-        exchange(1, up, (0, 1), faces)
+        exchange(1, up, (0, 1), along_x)
         exchange(2, kp, (1, 3), every_way)
     with jax.named_scope("weights2"):
         over(range(X0 + 11, X1 - 1), own_weights, 0, UW)
@@ -519,7 +538,8 @@
         scratch_shapes=[field] * 11 + [
             pltpu.VMEM((1, 128), F32),
             pltpu.VMEM((ngx * ngy, 128), F32),
-            sem.DMA((3, 4)), sem.DMA((4, 8)), sem.DMA((4, 8)), sem.DMA, sem.DMA, sem.REGULAR,
+            pltpu.VMEM((2, 2, 32, 4, 128), F32),
+            sem.DMA((2, 2, 4)), sem.DMA((3, 4)), sem.DMA((4, 8)), sem.DMA((4, 8)), sem.DMA, sem.DMA, sem.REGULAR,
         ],
         compiler_params=pltpu.CompilerParams(
             collective_id=0, has_side_effects=True, vmem_limit_bytes=50 * 2**20

time: 34 us -> 34.2 us (level)
  no operation moved by 1% of the time
where the time goes in v7:
time: 34.2 us; the launch traced here: 34 us
  Pallas kernels  30.9 us (90%)
  between operations  1.8 us (5%)
  local copies, waits for them, and re-layouts  1.32 us (4%)
    pallas_call x1, Pallas kernels, local(): pl.pallas_call(functools.partial(kernel, ngx, ngy), out_shape=(jax.ShapeD...  30.9 us
    unnamed x1, local copies, waits for them, and re-layouts  1.32 us

profile of v7, /device:TPU:1, one launch (start us, length us, event | category | flops | bytes accessed | tf_op | source)
XLA Modules:
  0.0 34.0 jit_solution(4322529390121581293)
XLA Ops:
  0.6 30.9 %shard_map.50 = (f32[32,32,512]{2,1,0:T(8,128)S(1)}, f32[1,128]{1,0:T(1,128)S(1)}) custom-call(f32[32,32,512]{2,1,0:T(8,128)} %rhs_hbm.1, f32[32,32,512]{2,1,0:T(8,128)} %x0_hbm.1, f32[32,32,512]{2,1,0:T(8,128)} %k_hbm.1), custom_call_target="tpu_custom_call" | custom-call | tf_op jit(solution)/shard_map/pallas_call | solution.py:533
  31.6 1.3 %copy.7 = f32[32,32,512]{2,1,0:T(8,128)} copy(f32[32,32,512]{2,1,0:T(8,128)S(1)} %get-tuple-element.8) | data formatting | bytes 4194304

commit v8 on v7

--- a/solution.py
+++ b/solution.py
@@ -83,14 +83,15 @@
     return tuple(y[0] / SCALE for y in (y1, y2, y3)), rest[0]
 
 
-def directions(gx, gy, ngx, ngy):
+def directions(gx, gy, ngx, ngy, reach=1):
     out = []
     for sx, sy in ((0, 1), (0, -1), (1, 0), (-1, 0), (1, 1), (1, -1), (-1, 1), (-1, -1)):
         to, come = [], []
         for step, at, n in ((sx, gx, ngx), (sy, gy, ngy)):
             if step:
-                to.append(at < n - 1 if step > 0 else at > 0)
-                come.append(at > 0 if step > 0 else at < n - 1)
+                low, high = at >= reach, at < n - reach
+                to.append(high if step > 0 else low)
+                come.append(low if step > 0 else high)
         both = (lambda c: c[0]) if len(to) == 1 else (lambda c: jnp.logical_and(*c))
         out.append((sx, sy, both(to), both(come)))
     return out
@@ -126,12 +127,20 @@
     gx, gy = lax.axis_index("gx"), lax.axis_index("gy")
     xs, ys = [lax.rem(gx + d, ngx) for d in range(ngx)], [lax.rem(gy + d, ngy) for d in range(ngy)]
     barrier = pltpu.get_barrier_semaphore()
-    near = [(0, 1), (0, ngy - 1), (1, 0), (ngx - 1, 0), (1, 1), (1, ngy - 1), (ngx - 1, 1), (ngx - 1, ngy - 1)]
-    greet = near + [(d, 0) for d in range(2, ngx - 1)] + [(0, d) for d in range(2, ngy - 1)]
-    for dx, dy in greet:
-        pl.semaphore_signal(
-            barrier, inc=1, device_id=(xs[dx], ys[dy]), device_id_type=MESH
-        )
+    def greet(sem, reach):
+        for sx, sy, to, _ in directions(gx, gy, ngx, ngy, reach):
+
+            @pl.when(to)
+            def _():
+                pl.semaphore_signal(
+                    sem, inc=1, device_id=(xs[sx * reach % ngx], ys[sy * reach % ngy]), device_id_type=MESH
+                )
+
+    def greeted(sem, reach):
+        senders = [jnp.where(come, 1, 0) for _, _, _, come in directions(gx, gy, ngx, ngy, reach)]
+        pl.semaphore_wait(sem, sum(senders[1:], senders[0]))
+
+    greet(barrier, 1)
     count = ngx * ngy
     loads = []
     for i, (src, dst) in enumerate(((k_hbm, kp), (x0_hbm, up), (rhs_hbm, rb))):
@@ -163,30 +172,6 @@
     fields = (kp, up, rp, v1, v2)
     zero = jnp.zeros((8, 128), F32)
 
-    for at, inside in ((0, has_low_x), (X1, has_high_x)):
-
-        @pl.when(jnp.logical_not(inside))
-        def _():
-            def fill(i, c):
-                for f in fields:
-                    for x in range(at, at + 3):
-                        f[x, pl.ds(pl.multiple_of(8 * i, 8), 8), :] = zero
-                return c
-
-            lax.fori_loop(0, ROWS // 8, fill, 0)
-
-    for at, inside in ((0, has_low_y), (R1, has_high_y)):
-
-        @pl.when(jnp.logical_not(inside))
-        def _():
-            def fill(x, c):
-                for f in fields:
-                    for r in (at, at + 8):
-                        f[x, r : r + 8, :] = zero
-                return c
-
-            lax.fori_loop(0, PLANES, fill, 0)
-
     def copy_of(e, f, layers, i):
         sx, sy = dirs[i][:2]
         return pltpu.make_async_remote_copy(
@@ -226,7 +211,7 @@
         for copy in face_loads[0]:
             copy.wait()
     with jax.named_scope("barrier"):
-        pl.semaphore_wait(barrier, len(greet))
+        greeted(barrier, 1)
         exchange(0, kp, (0, 1), along_y)
         for copy in face_loads[1]:
             copy.wait()
@@ -237,8 +222,31 @@
         exchange(0, kp, (0, 1), along_x)
         for copy in loads[8:]:
             copy.start()
-        for d in range(1, ngx):
-            pl.semaphore_signal(ready, inc=1, device_id=(xs[d], gy), device_id_type=MESH)
+        greet(ready.at[0], 1)
+
+    for at, inside in ((0, has_low_x), (X1, has_high_x)):
+
+        @pl.when(jnp.logical_not(inside))
+        def _():
+            def fill(i, c):
+                for f in fields:
+                    for x in range(at, at + 3):
+                        f[x, pl.ds(pl.multiple_of(8 * i, 8), 8), :] = zero
+                return c
+
+            lax.fori_loop(0, ROWS // 8, fill, 0)
+
+    for at, inside in ((0, has_low_y), (R1, has_high_y)):
+
+        @pl.when(jnp.logical_not(inside))
+        def _():
+            def fill(x, c):
+                for f in fields:
+                    for r in (at, at + 8):
+                        f[x, r : r + 8, :] = zero
+                return c
+
+            lax.fori_loop(0, PLANES, fill, 0)
 
     lane = lax.broadcasted_iota(jnp.int32, (8, 128), 1)
     sub = lax.broadcasted_iota(jnp.int32, (8, 128), 0)
@@ -360,6 +368,8 @@
         own_weights(X1 - 1, 0, with_x=False, diagonal=False)
         for copy in loads[8:]:
             copy.wait()
+        greeted(ready.at[0], 1)
+        greet(ready.at[1], 2)
 
     residual = step(up, rp, 1)
     m0 = (zero,)
@@ -404,6 +414,8 @@
 
     m0 = lax.cond(high_last, residual_strips((0, 1)), residual_strips((1, 0)), m0)
     exchange(3, rp, (0, 3), along_x)
+    greeted(ready.at[1], 2)
+    greet(ready.at[2], 4)
 
     powers = (step(rp, v1, 2), step(v1, v2, 2), step(v2, None, 2))
     rows = (chunks(1, 30), chunks(2, 29), chunks(3, 28))
@@ -412,6 +424,8 @@
     for n in range(3):
         with jax.named_scope("p2_in%d" % n):
             acc[n] = powers[n](range(X0 + depth[n], X1 - depth[n]), rows[n], acc[n], (U1, U2, U3)[n])
+    greeted(ready.at[2], 4)
+    greet(ready.at[3], 8)
     with jax.named_scope("wait_k2"):
         arrived(2, kp, (1, 3), every_way)
     with jax.named_scope("halo_weights"):
@@ -484,7 +498,7 @@
     place = gx * ngy + gy
     row[...] = mine
     gath[pl.ds(place, 1), :] = mine
-    pl.semaphore_wait(ready, ngx - 1)
+    greeted(ready.at[3], 8)
     with jax.named_scope("gsend"):
         for dx, dy in far_first(ngx, ngy):
             pltpu.make_async_remote_copy(
@@ -539,7 +553,7 @@
             pltpu.VMEM((1, 128), F32),
             pltpu.VMEM((ngx * ngy, 128), F32),
             pltpu.VMEM((2, 2, 32, 4, 128), F32),
-            sem.DMA((2, 2, 4)), sem.DMA((3, 4)), sem.DMA((4, 8)), sem.DMA((4, 8)), sem.DMA, sem.DMA, sem.REGULAR,
+            sem.DMA((2, 2, 4)), sem.DMA((3, 4)), sem.DMA((4, 8)), sem.DMA((4, 8)), sem.DMA, sem.DMA, sem.REGULAR((4,)),
         ],
         compiler_params=pltpu.CompilerParams(
             collective_id=0, has_side_effects=True, vmem_limit_bytes=50 * 2**20

time: 34.2 us -> 34 us (level)
  no operation moved by 1% of the time
where the time goes in v8:
time: 34 us; the launch traced here: 33.8 us
  Pallas kernels  30.7 us (90%)
  between operations  1.8 us (5%)
  local copies, waits for them, and re-layouts  1.32 us (4%)
    pallas_call x1, Pallas kernels, local(): pl.pallas_call(functools.partial(kernel, ngx, ngy), out_shape=(jax.ShapeD...  30.7 us
    unnamed x1, local copies, waits for them, and re-layouts  1.32 us

profile of v8, /device:TPU:1, one launch (start us, length us, event | category | flops | bytes accessed | tf_op | source)
XLA Modules:
  0.0 33.8 jit_solution(8555326343377427521)
XLA Ops:
  0.6 30.7 %shard_map.50 = (f32[32,32,512]{2,1,0:T(8,128)S(1)}, f32[1,128]{1,0:T(1,128)S(1)}) custom-call(f32[32,32,512]{2,1,0:T(8,128)} %rhs_hbm.1, f32[32,32,512]{2,1,0:T(8,128)} %x0_hbm.1, f32[32,32,512]{2,1,0:T(8,128)} %k_hbm.1), custom_call_target="tpu_custom_call" | custom-call | tf_op jit(solution)/shard_map/pallas_call | solution.py:547
  31.3 1.3 %copy.7 = f32[32,32,512]{2,1,0:T(8,128)} copy(f32[32,32,512]{2,1,0:T(8,128)S(1)} %get-tuple-element.8) | data formatting | bytes 4194304
